TPU v7x, 512 devices: a whole 4x8x8 slice. The times are simulated.
512 devices in a mesh: rep: 8 (over y), dp: 64 (over z, x, core).
Axes of the slice: x: 4, y: 8, z: 8, core: 2. Of those that a mesh axis runs over, the one named last changes fastest.
Arguments:
- hidden: bfloat16 [1024, 2, 3584], P(('rep', 'dp')), may hold values from -96 to 96
- lm_head: bfloat16 [3584, 196608], P(None, ('rep', 'dp')), may hold values from -0.3125 to 0.3125
- reward_head: bfloat16 [3584], replicated, may hold values from -0.09375 to 0.09375
- target_ids: int32 [1024, 2], P(('rep', 'dp')), may hold values from 0 to 196607
- lengths: int32 [1024], P(('rep', 'dp')), may hold values from 1 to 2
- prompt_ids: int32 [1024], P(('rep', 'dp')), may hold values from 0 to 63, as said below
Outputs:
- token_logprobs: float32 [1024, 2], P(('rep', 'dp'))
- advantages: float32 [1024], P(('rep', 'dp'))
Inputs may be any that keep to these rules, and one draw needn't show every extreme that they name: `prompt_ids`: each prompt id names exactly 16 responses.
All inputs are finite; a program needn't handle non-finite values.
Results may differ from a plain program's by a relative error of at most 0.0003.
Values may be sent and summed in bfloat16 or wider, within the bound.
A program may use at most 128 MiB of HBM per device.

v0:
```python
import functools

import jax
import jax.numpy as jnp
from jax import lax
from jax.sharding import Mesh
from jax.sharding import PartitionSpec as P

GROUP = 16
PROM_DEV = 1
DP = ("dp_0", "dp_1", "dp_2")
REP_DP = ("rep", "dp_0", "dp_1", "dp_2")


def over_axes(x, axes):
    return functools.reduce(lax.pmax, axes, x)


def over_axes_2(x, axes):
    return functools.reduce(lax.psum, axes, x)


def moments(stacked):
    means = stacked[0] / GROUP
    scales = jnp.sqrt(jnp.maximum(stacked[1] / GROUP - means * means, 1.0))
    return (means, scales)


def local(hidden, lm_head, reward_head, target_ids, lengths, prompt_ids):
    resp_dev, window, width = hidden.shape
    voc_dev = lm_head.shape[1]
    owners = lax.axis_size(DP)
    me = lax.axis_index("rep") * owners + lax.axis_index(DP)
    tok_dev = resp_dev * window
    all_ids = lax.all_gather(target_ids.reshape(tok_dev), REP_DP, axis=0, tiled=True)
    local_ids = all_ids - me * voc_dev
    columns = lax.broadcasted_iota(jnp.int32, (1, voc_dev), 1)
    piece = lax.all_gather(hidden, REP_DP, axis=0, tiled=True)
    count = piece.shape[0] * window
    flat = piece.reshape(count, width)
    logits = jnp.dot(flat, lm_head, preferred_element_type=jnp.float32)
    peak = jnp.max(logits, axis=1)
    total = jnp.sum(jnp.exp(logits - peak[:, None]), axis=1)
    picked = jnp.sum(jnp.where(columns == local_ids[:, None], logits, 0.0), axis=1)
    totals = total
    picks = picked
    first_own = me * tok_dev
    whole_top = over_axes(peak, REP_DP)
    scaled = totals * jnp.exp(peak - whole_top)
    whole_total, whole_pick = (over_axes_2(scaled, REP_DP), over_axes_2(picks, REP_DP))
    top = lax.dynamic_slice_in_dim(whole_top, first_own, tok_dev)
    total = lax.dynamic_slice_in_dim(whole_total, first_own, tok_dev)
    picked = lax.dynamic_slice_in_dim(whole_pick, first_own, tok_dev)
    logprob = (picked - (top + jnp.log(total))).reshape(resp_dev, window)
    positions = lax.broadcasted_iota(jnp.int32, (resp_dev, window), 1)
    token_logprobs = jnp.where(positions < lengths[:, None], logprob, 0.0)
    last = jnp.take_along_axis(hidden, (lengths - 1)[:, None, None], axis=1)[:, 0, :]
    rewards = jnp.dot(last, reward_head, preferred_element_type=jnp.float32)
    prompts = PROM_DEV * owners
    member = (prompt_ids[:, None] == lax.broadcasted_iota(jnp.int32, (1, prompts), 1)).astype(
        jnp.float32
    )
    sums = jnp.dot(rewards, member, precision=lax.Precision.HIGHEST)
    squares = jnp.dot(rewards * rewards, member, precision=lax.Precision.HIGHEST)
    stacked = jnp.stack([sums, squares])
    whole = over_axes_2(stacked, REP_DP)
    means, scales = moments(whole)
    centre = jnp.dot(member, means, precision=lax.Precision.HIGHEST)
    spread = jnp.dot(member, scales, precision=lax.Precision.HIGHEST)
    advantages = (rewards - centre) / spread
    return (token_logprobs, advantages)


def solution(mesh):
    split = Mesh(mesh.devices.reshape(mesh.shape["rep"], 8, 4, 2), ("rep", "dp_0", "dp_1", "dp_2"))
    placed = (P(REP_DP, None, None), P(None, REP_DP), P(), P(REP_DP, None), P(REP_DP), P(REP_DP))
    return jax.shard_map(
        local, mesh=split, in_specs=placed, out_specs=(P(REP_DP, None), P(REP_DP)), check_vma=False
    )
```

profile of v0, /device:TPU:1, one launch (start us, length us, event | category | flops | bytes accessed | tf_op | source)
XLA Modules:
  0.0 320.4 jit_solution(8423312800104367494)
XLA Ops:
  7.2 0.7 all-gather.2.cloned.1.call-update
  7.9 0.8 reshape.52
  8.8 0.7 reshape.54
  9.5 0.7 fusion.24
  10.4 1.4 gather_fusion
  11.8 0.3 dynamic-update-slice
  12.1 106.4 %all-reduce = s32[2048]{0:T(1024)S(1)} all-reduce(s32[2048]{0:T(1024)S(1)} %dynamic-update-slice), channel_id=1, replica_groups=mesh['rep'=8,'dp_0'=8,'dp_1'=4,'dp_2'=2] {'rep','dp_0','dp_1','dp_2'}, use_global_device_ids=true, to_apply=%add | all-reduce | flops 2048 | bytes 16384
  118.5 0.7 compare_and_fusion
  119.4 0.9 fusion.4
  120.3 0.8 fusion.5
  121.1 29.8 %all-gather.2.cloned.1.call-done = bf16[1024,2,3584]{2,1,0:T(2,128)(2,1)} async-done(((bf16[2,2,3584]{2,1,0:T(2,128)(2,1)}), bf16[1024,2,3584]{2,1,0:T(2,128)(2,1)}) %all-gather.2.cloned.1.call-update) | async-done | bytes 14680080 | tf_op jit(solution)/shard_map/all_gather | solution.py:38
  150.9 29.3 %reshape.41 = bf16[2048,3584]{1,0:T(8,128)(2,1)} reshape(bf16[1024,2,3584]{2,1,0:T(2,128)(2,1)} %all-gather.2.cloned.1.call-done) | data formatting | bytes 29360128 | tf_op jit(solution)/shard_map/reshape | solution.py:40
  180.2 11.0 %fusion.25 = (f32[2048]{0:T(1024)S(1)}, f32[2048,384]{0,1:T(8,128)}) fusion(bf16[2048,3584]{1,0:T(8,128)(2,1)} %reshape.41, bf16[3584,384]{1,0:T(8,128)(2,1)S(1)} %copy-done), kind=kOutput, calls=%fused_computation.44 | convolution fusion | flops 5637928960 | bytes 20586496 | tf_op jit(solution)/shard_map/dot_general | solution.py:41
  191.2 12.6 %pmax.28 = f32[2048]{0:T(1024)S(1)} all-reduce(f32[2048]{0:T(1024)S(1)} %get-tuple-element.16), channel_id=1, replica_groups=mesh['rep'=8,'dp_0'=8,'dp_1'=4,'dp_2'=2] {'rep'}, use_global_device_ids=true, to_apply=%region_6.7 | all-reduce | flops 2048 | bytes 16384 | tf_op jit(solution)/shard_map/pmax | solution.py:16
  203.9 12.6 %pmax.29 = f32[2048]{0:T(1024)S(1)} all-reduce(f32[2048]{0:T(1024)S(1)} %pmax.28), channel_id=1, replica_groups=mesh['rep'=8,'dp_0'=8,'dp_1'=4,'dp_2'=2] {'dp_0'}, use_global_device_ids=true, to_apply=%region_7.8 | all-reduce | flops 2048 | bytes 16384 | tf_op jit(solution)/shard_map/pmax | solution.py:16
  216.5 6.6 %pmax.30 = f32[2048]{0:T(1024)S(1)} all-reduce(f32[2048]{0:T(1024)S(1)} %pmax.29), channel_id=1, replica_groups=mesh['rep'=8,'dp_0'=8,'dp_1'=4,'dp_2'=2] {'dp_1'}, use_global_device_ids=true, to_apply=%region_8.9 | all-reduce | flops 2048 | bytes 16384 | tf_op jit(solution)/shard_map/pmax | solution.py:16
  223.1 11.8 %pmax.31 = f32[2048]{0:T(1024)S(1)} all-reduce(f32[2048]{0:T(1024)S(1)} %pmax.30), channel_id=1, replica_groups=mesh['rep'=8,'dp_0'=8,'dp_1'=4,'dp_2'=2] {'dp_2'}, use_global_device_ids=true, to_apply=%region_9.10 | all-reduce | flops 2048 | bytes 16384 | tf_op jit(solution)/shard_map/pmax | solution.py:16
  235.0 2.7 select_reduce_fusion
  237.7 20.9 %all-reduce.2 = (f32[2048]{0:T(1024)S(1)}, f32[2048]{0:T(1024)S(1)}, f32[2,64]{1,0:T(2,128)S(1)}) all-reduce(f32[2048]{0:T(1024)S(1)} %exponential_multiply_fusion, f32[2048]{0:T(1024)S(1)} %get-tuple-element.2, f32[2,64]{1,0:T(2,128)S(1)} %pad_maximum_fusion), channel_id=1, replica_groups=mesh['rep'=8,'dp_0'=8,'dp_1'=4,'dp_2'=2] {'rep'}, use_global_device_ids=true, to_apply=%region_11.12 | all-reduce | flops 4224 | bytes 33792 | tf_op jit(solution)/shard_map/psum | solution.py:20
  258.6 20.1 %all-reduce.1 = (f32[2048]{0:T(1024)S(1)}, f32[2048]{0:T(1024)S(1)}, f32[2,64]{1,0:T(2,128)S(1)}) all-reduce(f32[2048]{0:T(1024)S(1)} %get-tuple-element.7, f32[2048]{0:T(1024)S(1)} %get-tuple-element.8, f32[2,64]{1,0:T(2,128)S(1)} %get-tuple-element.9), channel_id=1, replica_groups=mesh['rep'=8,'dp_0'=8,'dp_1'=4,'dp_2'=2] {'dp_0'}, use_global_device_ids=true, to_apply=%region_12.13 | all-reduce | flops 4224 | bytes 33792 | tf_op jit(solution)/shard_map/psum | solution.py:20
  278.7 11.6 %all-reduce.3 = (f32[2048]{0:T(1024)S(1)}, f32[2048]{0:T(1024)S(1)}, f32[2,64]{1,0:T(2,128)S(1)}) all-reduce(f32[2048]{0:T(1024)S(1)} %get-tuple-element.4, f32[2048]{0:T(1024)S(1)} %get-tuple-element.5, f32[2,64]{1,0:T(2,128)S(1)} %get-tuple-element.6), channel_id=1, replica_groups=mesh['rep'=8,'dp_0'=8,'dp_1'=4,'dp_2'=2] {'dp_1'}, use_global_device_ids=true, to_apply=%region_13.14 | all-reduce | flops 4224 | bytes 33792 | tf_op jit(solution)/shard_map/psum | solution.py:20
  290.3 21.5 %all-reduce.4 = (f32[2048]{0:T(1024)S(1)}, f32[2048]{0:T(1024)S(1)}, f32[2,64]{1,0:T(2,128)S(1)}) all-reduce(f32[2048]{0:T(1024)S(1)} %get-tuple-element.10, f32[2048]{0:T(1024)S(1)} %get-tuple-element.11, f32[2,64]{1,0:T(2,128)S(1)} %get-tuple-element.12), channel_id=1, replica_groups=mesh['rep'=8,'dp_0'=8,'dp_1'=4,'dp_2'=2] {'dp_2'}, use_global_device_ids=true, to_apply=%region_14.15 | all-reduce | flops 4224 | bytes 33792 | tf_op jit(solution)/shard_map/psum | solution.py:20
  312.0 0.6 compare_select_fusion.1
  312.8 0.7 fusion.1
  (19 shorter events, 0.9 us)
Async XLA Ops:
  7.2 173.1 %copy-start = (bf16[3584,384]{1,0:T(8,128)(2,1)S(1)}, bf16[3584,384]{1,0:T(8,128)(2,1)}, u32[]{:S(2)}) copy-start(bf16[3584,384]{1,0:T(8,128)(2,1)} %param.7) | copy-start | bytes 8257540
  7.2 143.7 %all-gather.2.cloned.1.call-start = ((), (), s32[]{:S(2)}) async-start(), calls=%async_computation | async-start | bytes 14708736 | tf_op jit(solution)/shard_map/all_gather | solution.py:38
  191.2 120.8 %copy-start.1 = (s32[2]{0:T(128)S(1)}, s32[2]{0:T(128)}, u32[]{:S(2)}) copy-start(s32[2]{0:T(128)} %param.10) | copy-start | bytes 28
  191.2 121.4 %copy-start.2 = (s32[2]{0:T(128)S(1)}, s32[2]{0:T(128)}, u32[]{:S(2)}) copy-start(s32[2]{0:T(128)} %param.11) | copy-start | bytes 28
Sparse Core Ops, SparseCore 0:
  12.4 138.4 all-gather.1
where the time goes:
time: 322 us; the launch traced here: 320 us
  blocking collectives  224 us (70%)
  local copies, waits for them, and re-layouts  32.7 us (10%)
  waiting for transfers between devices  30.5 us (9%)
  between operations  14.1 us (4%)
  matrix products  13.8 us (4%)
  other arithmetic  4.98 us (2%)
    unnamed x1, blocking collectives  106 us
    psum x4, blocking collectives, over_axes_2(): return functools.reduce(lax.psum, axes, x)  74.1 us
    pmax x4, blocking collectives, over_axes(): return functools.reduce(lax.pmax, axes, x)  43.7 us
    all_gather x1, waiting for transfers between devices, local(): piece = lax.all_gather(hidden, REP_DP, axis=0, tiled=True)  29.8 us
    reshape x1, local copies, waits for them, and re-layouts, local(): flat = piece.reshape(count, width)  29.3 us
    dot_general x1, matrix products, local(): logits = jnp.dot(flat, lm_head, preferred_element_type=jnp.float32)  11 us
  transfers between devices with their start and end apart: 1, of which 1 were waited for; matrix products, arithmetic and copies ran while one was open for 2% of the time, Pallas kernels for 0%

commit v1 on v0

v1 whole, which is shorter than its diff:
```python
import functools

import jax
import jax.numpy as jnp
from jax import lax
from jax.experimental import pallas as pl
from jax.experimental.pallas import tpu as pltpu
from jax.sharding import Mesh
from jax.sharding import PartitionSpec as P

GROUP = 16
PROMPTS = 64
REP_DP = ("rep", "dp_0", "dp_1", "dp_2")
AXY, AXZ, AXX, AXC = REP_DP
LANES = 128
MESH = pl.DeviceIdType.MESH
F32 = jnp.float32


def ring_offsets(n):
    order = [0]
    for d in range(1, n // 2 + 1):
        order.append(-d)
        if 2 * d < n:
            order.append(d)
    return order


def hops(n, off):
    return min(off % n, -off % n)


def first_events(n):
    out = []
    for d in range(1, n // 2 + 1):
        out.append((d, 1))
        if 2 * d < n:
            out.append((d, -1))
    return out


def second_events(n1, n2):
    out = []
    for j in range(n1):
        for d in range(1, n2 // 2 + 1):
            if 2 * d < n2:
                out.append((j, d, 1))
                out.append((j, d, -1))
            else:
                out.append((j, d, 1 if j % 2 == 0 else -1))
    return out


def kernel(
    sizes, hid, whbm, rhead, ids, lens, pids, out1, out2,
    wmat, abuf, bbuf, acc, gath, gmeta, meta, tiles, got_z, got_y, got_x, sum_y, sum_x, pair, pgot,
    own_sem, w_send, w_recv, g_send, g_recv, m_send, m_recv, p_send, p_recv,
    a_send, a_recv, b_send, b_recv, z_send, z_recv, y_send, y_recv, x_send, x_recv,
):
    nx, ny, nz, ka, kb = sizes
    rows = nx * 4
    voc = whbm.shape[1]
    y, z, x, c = (lax.axis_index(a) for a in (AXY, AXZ, AXX, AXC))

    def at(pos, off, n):
        return lax.rem(pos + (off % n), n)

    own_w = pltpu.make_async_copy(whbm, wmat.at[:, pl.ds(0, voc)], own_sem)
    own_w.start()

    row8 = lax.broadcasted_iota(jnp.int32, (8, LANES), 0)
    lane8 = lax.broadcasted_iota(jnp.int32, (8, LANES), 1)
    idv = jnp.zeros((8, LANES), jnp.int32)
    for t in range(4):
        idv = jnp.where(row8 == t, ids[t // 2, t % 2], idv)
    digits = jnp.where(lane8 == 0, idv >> 16, jnp.where(lane8 == 1, (idv >> 8) & 255, idv & 255))
    meta[...] = jnp.where(lane8 < 3, digits, 0).astype(F32)

    barrier = pltpu.get_barrier_semaphore()
    partners = [{AXX: at(x, d, nx)} for d in range(1, nx)]
    partners += [{AXY: at(y, d, ny)} for d in (1, -1)]
    partners += [{AXZ: at(z, d, nz)} for d in (1, -1)]
    partners += [{AXC: 1 - c}]
    for dev in partners:
        pl.semaphore_signal(barrier, inc=1, device_id=dev, device_id_type=MESH)
    pl.semaphore_wait(barrier, len(partners))

    started = []

    def send(src, dst, ssem, rsem, dev):
        copy = pltpu.make_async_remote_copy(
            src_ref=src, dst_ref=dst, send_sem=ssem, recv_sem=rsem, device_id=dev, device_id_type=MESH
        )
        copy.start()
        started.append(copy)
        return copy

    for d in range(1, nx):
        send(hid, gath.at[x], g_send.at[d - 1], g_recv.at[d - 1], {AXX: at(x, d, nx)})
    for d in range(1, nx):
        send(meta, gmeta.at[x], m_send.at[d - 1], m_recv.at[d - 1], {AXX: at(x, d, nx)})
    send(whbm, wmat.at[:, pl.ds(voc, voc)], w_send, w_recv, {AXC: 1 - c})

    gath[x] = hid[...]
    gmeta[x] = meta[...]

    weight = rhead[...].astype(F32)
    rewards = []
    for r in range(2):
        both = jnp.sum(hid[r].astype(F32) * weight, axis=1, keepdims=True)
        rewards.append(jnp.where(lens[r] == 1, both[0:1], both[1:2]))
    lane1 = lax.broadcasted_iota(jnp.int32, (1, LANES), 1)
    stacked = jnp.zeros((1, LANES), F32)
    for r in range(2):
        stacked += jnp.where(lane1 == pids[r], rewards[r], 0.0)
        stacked += jnp.where(lane1 == pids[r] + PROMPTS, rewards[r] * rewards[r], 0.0)
    pair[...] = jnp.where(row8 == 3, stacked, 0.0)

    for d in range(1, nx):
        src = at(x, -d, nx)
        pltpu.make_async_copy(gath.at[src], gath.at[src], g_recv.at[d - 1]).wait()
        pltpu.make_async_copy(gmeta.at[src], gmeta.at[src], m_recv.at[d - 1]).wait()

    whole = jnp.concatenate(
        [gath[i, r].astype(F32) for i in range(nx) for r in range(2)], axis=0
    ).astype(jnp.bfloat16)
    for k in range(ka):
        abuf[y, z, k] = whole[:, k * LANES:(k + 1) * LANES]
    for k in range(kb):
        bbuf[y, z, k] = whole[:, (ka + k) * LANES:(ka + k + 1) * LANES]
    abuf[y, z, ka] = jnp.concatenate([gmeta[i, 0:4] for i in range(nx)], axis=0).astype(jnp.bfloat16)

    send(pair, pgot, p_send, p_recv, {AXC: 1 - c})

    class Colour:
        pass

    def colour(buf, first, p1, n1, axis1, p2, n2, axis2, ssem, rsem):
        col = Colour()
        offs = ring_offsets(n1)
        ev1, ev2 = first_events(n1), second_events(n1, n2)
        index1 = {e: i for i, e in enumerate(ev1)}
        index2 = {e: len(ev1) + i for i, e in enumerate(ev2)}

        def block(off1, off2):
            q1, q2 = at(p1, off1, n1), at(p2, off2, n2)
            return buf.at[q1, q2] if first else buf.at[q2, q1]

        def put1(d, way):
            if (d, way) in index1:
                i = index1[(d, way)]
                b = block(-way * (d - 1), 0)
                send(b, b, ssem.at[i], rsem.at[i], {axis1: at(p1, way, n1)})

        def put2(j, d, way):
            if (j, d, way) in index2:
                i = index2[(j, d, way)]
                b = block(offs[j], -way * (d - 1))
                send(b, b, ssem.at[i], rsem.at[i], {axis2: at(p2, way, n2)})

        def take(b, i):
            pltpu.make_async_copy(b, b, rsem.at[i]).wait()

        def begin():
            for way in (1, -1):
                put1(1, way)
            for way in (1, -1):
                put2(0, 1, way)

        def got1(d, way):
            take(block(-way * d, 0), index1[(d, way)])
            put1(d + 1, way)
            j = [o % n1 for o in offs].index(-way * d % n1)
            for w2 in (1, -1):
                put2(j, 1, w2)

        def got2(j, d, way):
            take(block(offs[j], -way * d), index2[(j, d, way)])
            put2(j, d + 1, way)

        col.begin = begin
        col.events = [(e[0], 0, functools.partial(got1, *e)) for e in ev1]
        col.events += [
            (hops(n1, offs[e[0]]) + e[1], 1, functools.partial(got2, *e))
            for e in sorted(ev2, key=lambda e: (hops(n1, offs[e[0]]) + e[1], e[1], e[0]))
        ]
        return col

    first = colour(abuf, True, y, ny, AXY, z, nz, AXZ, a_send, a_recv)
    second = colour(bbuf, False, z, nz, AXZ, y, ny, AXY, b_send, b_recv)
    first.begin()
    second.begin()
    acc[...] = jnp.zeros_like(acc)

    wide = 2 * LANES if (2 * voc) % (2 * LANES) == 0 else LANES

    def multiply(is_first, positions):
        buf, nk, k0, n1 = (abuf, ka, 0, ny) if is_first else (bbuf, kb, ka, nz)

        def step(n, carry):
            cols = pl.ds(pl.multiple_of(n * wide, wide), wide)
            left = []
            for q in positions:
                parts = [
                    (buf[:, q, k] if is_first else buf[q, :, k]).reshape(n1 * rows, LANES)
                    for k in range(nk)
                ]
                left.append(jnp.concatenate(parts, axis=1))
            left = jnp.concatenate(left, axis=0) if len(left) > 1 else left[0]
            right = wmat[pl.ds(k0 * LANES, nk * LANES), cols]
            part = jnp.dot(left, right, preferred_element_type=F32)
            for i, q in enumerate(positions):
                piece = part[i * n1 * rows:(i + 1) * n1 * rows].reshape(n1, rows, wide)
                if is_first:
                    acc[:, q, :, cols] += piece
                else:
                    acc[q, :, :, cols] += piece
            return carry

        lax.fori_loop(0, 2 * voc // wide, step, 0)

    waves = ny // 2 + nz // 2
    waited = False
    for wave in range(1, waves + 1):
        for kind in (0, 1):
            mine = [[e for e in col.events if e[0] == wave and e[1] == kind] for col in (first, second)]
            for i in range(max(len(m) for m in mine)):
                for m in mine:
                    if i < len(m):
                        m[i][2]()
        for is_first, n1, n2, p2 in ((True, ny, nz, z), (False, nz, ny, y)):
            d = wave - n1 // 2
            if 0 <= d <= n2 // 2:
                if not waited:
                    own_w.wait()
                    pltpu.make_async_copy(whbm, wmat.at[:, pl.ds(voc, voc)], w_recv).wait()
                    waited = True
                where = [at(p2, d, n2)]
                if 0 < d and 2 * d < n2:
                    where.append(at(p2, -d, n2))
                multiply(is_first, where)

    pltpu.make_async_copy(pgot, pgot, p_recv).wait()
    prompt_row = pair[...] + pgot[...]
    chip = ((y * nz + z) * nx + x) * 2
    toks = ny * rows
    lane = lax.broadcasted_iota(jnp.int32, (toks, 2 * voc), 1)
    entry = jnp.where(lane < voc, (chip + c) * voc + lane, (chip + 1 - c) * voc + lane - voc)
    lane_t = lax.broadcasted_iota(jnp.int32, (toks, LANES), 1)

    def slab(q):
        logits = acc[:, q].reshape(toks, 2 * voc)
        peak = jnp.max(logits, axis=1, keepdims=True)
        total = jnp.sum(jnp.exp(logits - peak), axis=1, keepdims=True)
        dig = abuf[:, q, ka].reshape(toks, LANES).astype(F32)
        want = (dig[:, 0:1] * 65536.0 + dig[:, 1:2] * 256.0 + dig[:, 2:3]).astype(jnp.int32)
        picked = jnp.sum(jnp.where(entry == want, logits, 0.0), axis=1, keepdims=True)
        side = jnp.where(lane_t == 0, peak, jnp.where(lane_t == 1, total, jnp.where(lane_t == 2, picked, 0.0)))
        if toks < LANES:
            side = jnp.concatenate([side, jnp.zeros((LANES - toks, LANES), F32)], axis=0)
        return jnp.where(row8 == 3, prompt_row, side.T[0:8, :])

    def step(i, carry):
        h = (i + 1) // 2
        d = nz // 2 + h * (1 - 2 * (i % 2))
        q = lax.rem(z + d, nz)
        tiles[i] = slab(q)
        pltpu.make_async_remote_copy(
            src_ref=tiles.at[i], dst_ref=got_z.at[i], send_sem=z_send.at[i], recv_sem=z_recv.at[i],
            device_id={AXZ: q}, device_id_type=MESH,
        ).start()
        return carry

    lax.fori_loop(0, nz - 1, step, 0)

    def merge(parts):
        top = functools.reduce(jnp.maximum, [p[0:1] for p in parts])
        out = sum(p * jnp.where(row8 == 1, jnp.exp(p[0:1] - top), 1.0) for p in parts)
        return jnp.where(row8 == 0, top, out)

    mine = slab(z)
    for i in range(nz - 1):
        pltpu.make_async_copy(got_z.at[i], got_z.at[i], z_recv.at[i]).wait()
    sum_y[...] = merge([mine] + [got_z[i] for i in range(nz - 1)])
    far = sorted(range(1, ny), key=lambda d: -hops(ny, d))
    for d in far:
        send(sum_y, got_y.at[d - 1], y_send.at[d - 1], y_recv.at[d - 1], {AXY: at(y, d, ny)})
    for d in reversed(far):
        pltpu.make_async_copy(got_y.at[d - 1], got_y.at[d - 1], y_recv.at[d - 1]).wait()
    sum_x[...] = merge([sum_y[...]] + [got_y[d - 1] for d in range(1, ny)])
    far = sorted(range(1, nx), key=lambda d: -hops(nx, d))
    for d in far:
        send(sum_x, got_x.at[d - 1], x_send.at[d - 1], x_recv.at[d - 1], {AXX: at(x, d, nx)})
    for d in reversed(far):
        pltpu.make_async_copy(got_x.at[d - 1], got_x.at[d - 1], x_recv.at[d - 1]).wait()
    done = merge([sum_x[...]] + [got_x[d - 1] for d in range(1, nx)])

    logprob = done[2:3] - (done[0:1] + jnp.log(done[1:2]))
    base = y * rows + x * 4
    r_out = lax.broadcasted_iota(jnp.int32, (2, 2), 0)
    w_out = lax.broadcasted_iota(jnp.int32, (2, 2), 1)
    value = jnp.zeros((2, 2), F32)
    for t in range(4):
        r, w = t // 2, t % 2
        one = jnp.sum(jnp.where(lane1 == base + t, logprob, 0.0), axis=1, keepdims=True)
        one = jnp.where(w < lens[r], one, 0.0)
        value = jnp.where((r_out == r) & (w_out == w), one, value)
    out1[...] = value
    moment = done[3:4] * (1.0 / GROUP)
    spot = lax.broadcasted_iota(jnp.int32, (1, 2), 1)
    adv = jnp.zeros((1, 2), F32)
    for r in range(2):
        mean = jnp.sum(jnp.where(lane1 == pids[r], moment, 0.0), axis=1, keepdims=True)
        square = jnp.sum(jnp.where(lane1 == pids[r] + PROMPTS, moment, 0.0), axis=1, keepdims=True)
        scale = jnp.sqrt(jnp.maximum(square - mean * mean, 1.0))
        adv = jnp.where(spot == r, (rewards[r] - mean) / scale, adv)
    out2[...] = adv

    for copy in started:
        copy.wait_send()
    for i in range(nz - 1):
        pltpu.make_async_copy(tiles.at[i], tiles.at[i], z_send.at[i]).wait()


def local(hidden, lm_head, reward_head, target_ids, lengths, prompt_ids):
    nx, ny, nz = (lax.axis_size(a) for a in (AXX, AXY, AXZ))
    width, voc = lm_head.shape
    tiles = width // LANES
    ka = tiles // 2
    kb = tiles - ka
    rows = nx * 4
    count_a = len(first_events(ny)) + len(second_events(ny, nz))
    count_b = len(first_events(nz)) + len(second_events(nz, ny))
    dma = pltpu.SemaphoreType.DMA
    vmem = pl.BlockSpec(memory_space=pltpu.VMEM)
    smem = pl.BlockSpec(memory_space=pltpu.SMEM)
    tile = (8, LANES)
    out1, out2 = pl.pallas_call(
        functools.partial(kernel, (nx, ny, nz, ka, kb)),
        out_shape=(jax.ShapeDtypeStruct((2, 2), F32), jax.ShapeDtypeStruct((1, 2), F32)),
        in_specs=[vmem, pl.BlockSpec(memory_space=pl.ANY), vmem, smem, smem, smem],
        out_specs=(vmem, vmem),
        scratch_shapes=[
            pltpu.VMEM((width, 2 * voc), jnp.bfloat16),
            pltpu.VMEM((ny, nz, ka + 1, rows, LANES), jnp.bfloat16),
            pltpu.VMEM((ny, nz, kb, rows, LANES), jnp.bfloat16),
            pltpu.VMEM((ny, nz, rows, 2 * voc), F32),
            pltpu.VMEM((nx, 2, 2, width), jnp.bfloat16),
            pltpu.VMEM((nx,) + tile, F32),
            pltpu.VMEM(tile, F32),
            pltpu.VMEM((nz - 1,) + tile, F32),
            pltpu.VMEM((nz - 1,) + tile, F32),
            pltpu.VMEM((ny - 1,) + tile, F32),
            pltpu.VMEM((nx - 1,) + tile, F32),
            pltpu.VMEM(tile, F32),
            pltpu.VMEM(tile, F32),
            pltpu.VMEM(tile, F32),
            pltpu.VMEM(tile, F32),
            dma, dma, dma,
            dma((nx - 1,)), dma((nx - 1,)), dma((nx - 1,)), dma((nx - 1,)),
            dma, dma,
            dma((count_a,)), dma((count_a,)), dma((count_b,)), dma((count_b,)),
            dma((nz - 1,)), dma((nz - 1,)), dma((ny - 1,)), dma((ny - 1,)), dma((nx - 1,)), dma((nx - 1,)),
        ],
        compiler_params=pltpu.CompilerParams(collective_id=0, has_side_effects=True),
        name="gather_score",
    )(hidden, lm_head, reward_head.reshape(1, width), target_ids, lengths, prompt_ids)
    return out1, out2.reshape(2)


def solution(mesh):
    split = Mesh(mesh.devices.reshape(mesh.shape["rep"], 8, 4, 2), REP_DP)
    placed = (P(REP_DP, None, None), P(None, REP_DP), P(), P(REP_DP, None), P(REP_DP), P(REP_DP))
    return jax.shard_map(
        local, mesh=split, in_specs=placed, out_specs=(P(REP_DP, None), P(REP_DP)), check_vma=False
    )
```

time: 322 us -> 90.2 us (0.28)
  the two profiles are of different devices: /device:TPU:1 before, /device:TPU:8 now
where the time goes in v1:
time: 90.2 us; the launch traced here: 89.9 us
  Pallas kernels  85.6 us (95%)
  local copies, waits for them, and re-layouts  3.7 us (4%)
    pallas_call x1, Pallas kernels, local(): pl.pallas_call(functools.partial(kernel, (nx, ny, nz, ka, kb)), out_shape...  85.6 us
    unnamed x2, local copies, waits for them, and re-layouts  2.39 us

profile of v1, /device:TPU:8, one launch (start us, length us, event | category | flops | bytes accessed | tf_op | source)
XLA Modules:
  0.0 89.9 jit_solution(6180440701487814963)
XLA Ops:
  0.6 1.3 %reshape.10.rhead = bf16[1,3584]{1,0:T(2,128)(2,1)} reshape(bf16[3584]{0:T(1024)(128)(2,1)} %param.8) | data formatting | bytes 14336 | tf_op jit(solution)/shard_map/reshape | solution.py:367
  1.9 85.6 %gather_score.1 = (f32[2,2]{1,0:T(2,128)}, f32[1,2]{1,0:T(1,128)}) custom-call(bf16[2,2,3584]{2,1,0:T(2,128)(2,1)} %hid.1, bf16[3584,384]{1,0:T(8,128)(2,1)} %whbm.1, bf16[1,3584]{1,0:T(2,128)(2,1)} %reshape.10.rhead, s32[2,2]{1,0:T(2,128)} %ids.1, s32[2]{0:T(128)} %lens.1, s32[2]{0:T(128)} %pids.1), custom_call_target="tpu_custom_call" | custom-call | tf_op jit(solution)/shard_map/gather_score/pallas_call | solution.py:338
  87.5 1.2 %copy.10 = f32[2,2]{1,0:T(2,128)} copy(f32[2,2]{1,0:T(2,128)} %get-tuple-element.8) | data formatting | bytes 32
  88.8 1.2 %copy.11 = f32[2]{0:T(128)} copy(f32[2]{0:T(128)} %bitcast.1) | data formatting | bytes 16

commit v2 on v1

v2 whole, which is shorter than its diff:
```python
import functools

import jax
import jax.numpy as jnp
from jax import lax
from jax.experimental import pallas as pl
from jax.experimental.pallas import tpu as pltpu
from jax.sharding import Mesh
from jax.sharding import PartitionSpec as P

GROUP = 16
PROMPTS = 64
REP_DP = ("rep", "dp_0", "dp_1", "dp_2")
AXY, AXZ, AXX, AXC = REP_DP
LANES = 128
MESH = pl.DeviceIdType.MESH
F32 = jnp.float32


def ring_offsets(n):
    order = [0]
    for d in range(1, n // 2 + 1):
        order.append(-d)
        if 2 * d < n:
            order.append(d)
    return order


def hops(n, off):
    return min(off % n, -off % n)


def first_events(n):
    out = []
    for d in range(1, n // 2 + 1):
        out.append((d, 1))
        if 2 * d < n:
            out.append((d, -1))
    return out


def second_events(n1, n2):
    out = []
    for j in range(n1):
        for d in range(1, n2 // 2 + 1):
            if 2 * d < n2:
                out.append((j, d, 1))
                out.append((j, d, -1))
            else:
                out.append((j, d, 1 if j % 2 == 0 else -1))
    return out


def groups_of(ny, nz):
    every = [(dy, dz) for dy in ring_offsets(ny) for dz in ring_offsets(nz)]
    return sorted(every, key=lambda g: hops(ny, g[0]) + hops(nz, g[1]))


def kernel(
    sizes, hid_in, whbm, rhead_in, ids_in, lens_in, pids_in, out1, out2,
    hid, rhead, ids, lens, pids,
    wmat, abuf, bbuf, cbuf, quarter, acc, side, gath, gmeta, meta, tiles, got_z, got_y, got_x, sum_y, sum_x, pair, pgot,
    in_sem, w_send, w_recv, g_send, g_recv, m_send, m_recv, p_send, p_recv,
    a_send, a_recv, b_send, b_recv, c_send, c_recv, z_send, z_recv, y_send, y_recv, x_send, x_recv,
):
    nx, ny, nz, ka, kb, kq = sizes
    rows = nx * 4
    voc = whbm.shape[1]
    y, z, x, c = (lax.axis_index(a) for a in (AXY, AXZ, AXX, AXC))

    def at(pos, off, n):
        return lax.rem(pos + (off % n), n)

    barrier = pltpu.get_barrier_semaphore()
    partners = [{AXX: at(x, d, nx)} for d in range(1, nx)]
    partners += [{AXY: at(y, d, ny)} for d in (1, -1)]
    partners += [{AXZ: at(z, d, nz)} for d in (1, -1)]
    partners += [{AXC: 1 - c}]
    for dev in partners:
        pl.semaphore_signal(barrier, inc=1, device_id=dev, device_id_type=MESH)

    loads = [
        pltpu.make_async_copy(src, dst, in_sem.at[i])
        for i, (src, dst) in enumerate((
            (hid_in, hid), (ids_in, ids), (lens_in, lens), (pids_in, pids), (rhead_in, rhead),
            (whbm, wmat.at[:, pl.ds(0, voc)]),
        ))
    ]
    for load in loads:
        load.start()
    loads[0].wait()
    loads[1].wait()

    row8 = lax.broadcasted_iota(jnp.int32, (8, LANES), 0)
    lane8 = lax.broadcasted_iota(jnp.int32, (8, LANES), 1)
    idv = jnp.zeros((8, LANES), jnp.int32)
    for t in range(4):
        idv = jnp.where(row8 == t, ids[t // 2, t % 2], idv)
    digits = jnp.where(lane8 == 0, idv >> 16, jnp.where(lane8 == 1, (idv >> 8) & 255, idv & 255))
    meta[...] = jnp.where(lane8 < 3, digits, 0).astype(F32)
    pl.semaphore_wait(barrier, len(partners))

    started = []

    def send(src, dst, ssem, rsem, dev, keep=True):
        copy = pltpu.make_async_remote_copy(
            src_ref=src, dst_ref=dst, send_sem=ssem, recv_sem=rsem, device_id=dev, device_id_type=MESH
        )
        copy.start()
        if keep:
            started.append(copy)

    def take(ref, sem):
        pltpu.make_async_copy(ref, ref, sem).wait()

    for d in range(1, nx):
        send(hid, gath.at[x], g_send.at[d - 1], g_recv.at[d - 1], {AXX: at(x, d, nx)})
    for d in range(1, nx):
        send(meta, gmeta.at[x], m_send.at[d - 1], m_recv.at[d - 1], {AXX: at(x, d, nx)})
    send(whbm, wmat.at[:, pl.ds(voc, voc)], w_send, w_recv, {AXC: 1 - c})

    gath[x] = hid[...]
    gmeta[x] = meta[...]

    for load in loads[2:5]:
        load.wait()
    rewards = []
    for r in range(2):
        both = sum(
            hid[r, :, pl.ds(k * LANES, LANES)].astype(F32) * rhead[k:k + 1].astype(F32)
            for k in range(rhead.shape[0])
        )
        both = jnp.sum(both, axis=1, keepdims=True)
        rewards.append(jnp.where(lens[r] == 1, both[0:1], both[1:2]))
    lane1 = lax.broadcasted_iota(jnp.int32, (1, LANES), 1)
    stacked = jnp.zeros((1, LANES), F32)
    for r in range(2):
        stacked += jnp.where(lane1 == pids[r], rewards[r], 0.0)
        stacked += jnp.where(lane1 == pids[r] + PROMPTS, rewards[r] * rewards[r], 0.0)
    pair[...] = jnp.where(row8 == 3, stacked, 0.0)

    for d in range(1, nx):
        src = at(x, -d, nx)
        take(gath.at[src], g_recv.at[d - 1])
        take(gmeta.at[src], m_recv.at[d - 1])

    whole = jnp.concatenate(
        [gath[i, r].astype(F32) for i in range(nx) for r in range(2)], axis=0
    ).astype(jnp.bfloat16)
    pieces = [whole[:, k * LANES:(k + 1) * LANES] for k in range(ka + kb + nx * kq)]
    for k in range(nx * kq):
        quarter[k // kq, k % kq] = pieces[ka + kb + k]
    for k in range(ka):
        abuf[y, z, k] = pieces[k]
    for k in range(kb):
        bbuf[y, z, k] = pieces[ka + k]
    abuf[y, z, ka] = jnp.concatenate([gmeta[i, 0:4] for i in range(nx)], axis=0).astype(jnp.bfloat16)
    for k in range(kq):
        abuf[y, z, ka + 1 + k] = quarter[x, k]

    send(pair, pgot, p_send, p_recv, {AXC: 1 - c})

    groups = groups_of(ny, nz)
    many = len(groups)
    place = {(dy % ny, dz % nz): i for i, (dy, dz) in enumerate(groups)}
    far_of = [hops(ny, dy) + hops(nz, dz) for dy, dz in groups]
    where = [(at(y, dy, ny), at(z, dz, nz)) for dy, dz in groups]

    def spread(i):
        for n, way in enumerate((1, -1)):
            send(
                abuf.at[where[i] + (pl.ds(ka + 1, kq),)], cbuf.at[(n,) + where[i]],
                c_send, c_recv.at[n * many + i], {AXX: at(x, way, nx)}, keep=False,
            )

    def spread_on(i):
        for n in range(2):
            take(cbuf.at[(n,) + where[i]], c_recv.at[n * many + i])
        n = i % 2
        send(
            cbuf.at[(n,) + where[i]], cbuf.at[(2,) + where[i]],
            c_send, c_recv.at[2 * many + i], {AXX: at(x, 1 - 2 * n, nx)}, keep=False,
        )

    def colour(buf, first, p1, n1, axis1, p2, n2, axis2, ssem, rsem):
        offs = ring_offsets(n1)
        ev1, ev2 = first_events(n1), second_events(n1, n2)
        index1 = {e: i for i, e in enumerate(ev1)}
        index2 = {e: len(ev1) + i for i, e in enumerate(ev2)}

        def block(off1, off2):
            i = place[(off1 % n1, off2 % n2) if first else (off2 % n2, off1 % n1)]
            return i, buf.at[where[i]]

        def put1(d, way):
            if (d, way) in index1:
                i = index1[(d, way)]
                b = block(-way * (d - 1), 0)[1]
                send(b, b, ssem.at[i], rsem.at[i], {axis1: at(p1, way, n1)})

        def put2(j, d, way):
            if (j, d, way) in index2:
                i = index2[(j, d, way)]
                b = block(offs[j], -way * (d - 1))[1]
                send(b, b, ssem.at[i], rsem.at[i], {axis2: at(p2, way, n2)})

        def begin():
            for way in (1, -1):
                put1(1, way)
            for way in (1, -1):
                put2(0, 1, way)
            if first:
                spread(0)

        def got1(d, way):
            i, b = block(-way * d, 0)
            take(b, rsem.at[index1[(d, way)]])
            put1(d + 1, way)
            j = [o % n1 for o in offs].index(-way * d % n1)
            for w2 in (1, -1):
                put2(j, 1, w2)
            if first:
                spread(i)

        def got2(j, d, way):
            i, b = block(offs[j], -way * d)
            take(b, rsem.at[index2[(j, d, way)]])
            put2(j, d + 1, way)
            if first:
                spread(i)

        events = [(e[0], 0, functools.partial(got1, *e)) for e in ev1]
        events += [
            (hops(n1, offs[e[0]]) + e[1], 1, functools.partial(got2, *e))
            for e in sorted(ev2, key=lambda e: (hops(n1, offs[e[0]]) + e[1], e[1], e[0]))
        ]
        return begin, events

    begin_a, events_a = colour(abuf, True, y, ny, AXY, z, nz, AXZ, a_send, a_recv)
    begin_b, events_b = colour(bbuf, False, z, nz, AXZ, y, ny, AXY, b_send, b_recv)
    begin_a()
    begin_b()

    wide = 2 * LANES
    chip = ((y * nz + z) * nx + x) * 2
    turns = [at(x, off, nx) for off in (0, -1, 1, 2)]
    starts = [pl.multiple_of((ka + kb + q * kq) * LANES, LANES) for q in turns]

    def product(chunk, last):
        def step(n, carry):
            cols = pl.ds(pl.multiple_of(n * wide, wide), wide)
            left = []
            for i in chunk:
                if last:
                    parts = [abuf[where[i] + (ka + 1 + k,)] for k in range(kq)]
                    parts += [cbuf[(r,) + where[i] + (k,)] for r in range(3) for k in range(kq)]
                else:
                    parts = [abuf[where[i] + (k,)] for k in range(ka)]
                    parts += [bbuf[where[i] + (k,)] for k in range(kb)]
                left.append(jnp.concatenate(parts, axis=1))
            left = jnp.concatenate(left, axis=0)
            if last:
                right = jnp.concatenate([wmat[pl.ds(s, kq * LANES), cols] for s in starts], axis=0)
            else:
                right = wmat[pl.ds(0, (ka + kb) * LANES), cols]
            part = jnp.dot(left, right, preferred_element_type=F32)
            for m, i in enumerate(chunk):
                piece = part[m * rows:(m + 1) * rows]
                if last:
                    piece = acc[where[i] + (slice(None), cols)] + piece
                acc[where[i] + (slice(None), cols)] = piece
            return carry

        lax.fori_loop(0, 2 * voc // wide, step, 0)

    def score(chunk):
        toks = len(chunk) * rows

        def logits():
            return jnp.concatenate([acc[where[i]] for i in chunk], axis=0)

        lane = lax.broadcasted_iota(jnp.int32, (toks, 2 * voc), 1)
        entry = jnp.where(lane < voc, (chip + c) * voc + lane, (chip + 1 - c) * voc + lane - voc)
        lane_t = lax.broadcasted_iota(jnp.int32, (toks, LANES), 1)
        peak = jnp.max(logits(), axis=1, keepdims=True)
        total = jnp.sum(jnp.exp(logits() - peak), axis=1, keepdims=True)
        dig = jnp.concatenate([abuf[where[i] + (ka,)] for i in chunk], axis=0).astype(F32)
        want = (dig[:, 0:1] * 65536.0 + dig[:, 1:2] * 256.0 + dig[:, 2:3]).astype(jnp.int32)
        picked = jnp.sum(jnp.where(entry == want, logits(), 0.0), axis=1, keepdims=True)
        out = jnp.where(lane_t == 0, peak, jnp.where(lane_t == 1, total, jnp.where(lane_t == 2, picked, 0.0)))
        for m, i in enumerate(chunk):
            side[where[i][1], where[i][0]] = out[m * rows:(m + 1) * rows]

    cuts = [0, many // 4, many // 2, 3 * many // 4, 7 * many // 8, many]
    chunks = [list(range(s, e)) for s, e in zip(cuts[:-1], cuts[1:])]
    whole_part, last_part = list(chunks), list(chunks)
    spread_wait = list(range(many))
    waves = ny // 2 + nz // 2
    ready = False
    for wave in range(1, waves + 3):
        for kind in (0, 1):
            mine = [[e for e in ev if e[0] == wave and e[1] == kind] for ev in (events_a, events_b)]
            for n in range(max(len(m) for m in mine)):
                for m in mine:
                    if n < len(m):
                        m[n][2]()
        for i in [i for i in spread_wait if far_of[i] < wave]:
            spread_on(i)
            spread_wait.remove(i)
        while whole_part and max(far_of[i] for i in whole_part[0]) <= wave:
            if not ready:
                loads[5].wait()
                take(wmat.at[:, pl.ds(voc, voc)], w_recv)
                ready = True
            product(whole_part.pop(0), False)
        while last_part and max(far_of[i] for i in last_part[0]) <= wave - 2:
            chunk = last_part.pop(0)
            for i in chunk:
                take(cbuf.at[(2,) + where[i]], c_recv.at[2 * many + i])
            product(chunk, True)
            score(chunk)

    take(pgot, p_recv)
    prompt_row = pair[...] + pgot[...]

    def slab(q):
        block = side[q].reshape(ny * rows, LANES)
        if ny * rows < LANES:
            block = jnp.concatenate([block, jnp.zeros((LANES - ny * rows, LANES), F32)], axis=0)
        return jnp.where(row8 == 3, prompt_row, block.T[0:8, :])

    def step(i, carry):
        h = (i + 1) // 2
        d = nz // 2 + h * (1 - 2 * (i % 2))
        q = lax.rem(z + d, nz)
        tiles[i] = slab(q)
        pltpu.make_async_remote_copy(
            src_ref=tiles.at[i], dst_ref=got_z.at[i], send_sem=z_send.at[i], recv_sem=z_recv.at[i],
            device_id={AXZ: q}, device_id_type=MESH,
        ).start()
        return carry

    lax.fori_loop(0, nz - 1, step, 0)

    def merge(parts):
        top = functools.reduce(jnp.maximum, [p[0:1] for p in parts])
        out = sum(p * jnp.where(row8 == 1, jnp.exp(p[0:1] - top), 1.0) for p in parts)
        return jnp.where(row8 == 0, top, out)

    mine = slab(z)
    for i in range(nz - 1):
        pltpu.make_async_copy(got_z.at[i], got_z.at[i], z_recv.at[i]).wait()
    sum_y[...] = merge([mine] + [got_z[i] for i in range(nz - 1)])
    far = sorted(range(1, ny), key=lambda d: -hops(ny, d))
    for d in far:
        send(sum_y, got_y.at[d - 1], y_send.at[d - 1], y_recv.at[d - 1], {AXY: at(y, d, ny)})
    for d in reversed(far):
        pltpu.make_async_copy(got_y.at[d - 1], got_y.at[d - 1], y_recv.at[d - 1]).wait()
    sum_x[...] = merge([sum_y[...]] + [got_y[d - 1] for d in range(1, ny)])
    far = sorted(range(1, nx), key=lambda d: -hops(nx, d))
    for d in far:
        send(sum_x, got_x.at[d - 1], x_send.at[d - 1], x_recv.at[d - 1], {AXX: at(x, d, nx)})
    for d in reversed(far):
        pltpu.make_async_copy(got_x.at[d - 1], got_x.at[d - 1], x_recv.at[d - 1]).wait()
    done = merge([sum_x[...]] + [got_x[d - 1] for d in range(1, nx)])

    logprob = done[2:3] - (done[0:1] + jnp.log(done[1:2]))
    base = y * rows + x * 4
    r_out = lax.broadcasted_iota(jnp.int32, (2, 2), 0)
    w_out = lax.broadcasted_iota(jnp.int32, (2, 2), 1)
    value = jnp.zeros((2, 2), F32)
    for t in range(4):
        r, w = t // 2, t % 2
        one = jnp.sum(jnp.where(lane1 == base + t, logprob, 0.0), axis=1, keepdims=True)
        one = jnp.where(w < lens[r], one, 0.0)
        value = jnp.where((r_out == r) & (w_out == w), one, value)
    out1[...] = value
    moment = done[3:4] * (1.0 / GROUP)
    spot = lax.broadcasted_iota(jnp.int32, (1, 2), 1)
    adv = jnp.zeros((1, 2), F32)
    for r in range(2):
        mean = jnp.sum(jnp.where(lane1 == pids[r], moment, 0.0), axis=1, keepdims=True)
        square = jnp.sum(jnp.where(lane1 == pids[r] + PROMPTS, moment, 0.0), axis=1, keepdims=True)
        scale = jnp.sqrt(jnp.maximum(square - mean * mean, 1.0))
        adv = jnp.where(spot == r, (rewards[r] - mean) / scale, adv)
    out2[...] = adv

    for copy in started:
        copy.wait_send()
    take(cbuf, c_send)
    for i in range(nz - 1):
        pltpu.make_async_copy(tiles.at[i], tiles.at[i], z_send.at[i]).wait()


def local(hidden, lm_head, reward_head, target_ids, lengths, prompt_ids):
    nx, ny, nz = (lax.axis_size(a) for a in (AXX, AXY, AXZ))
    width, voc = lm_head.shape
    tiles = width // LANES
    kq = max(1, tiles * 3 // (7 * nx))
    ka = (tiles - kq * nx) * 3 // 8
    kb = tiles - kq * nx - ka
    rows = nx * 4
    count_a = len(first_events(ny)) + len(second_events(ny, nz))
    count_b = len(first_events(nz)) + len(second_events(nz, ny))
    dma = pltpu.SemaphoreType.DMA
    vmem = pl.BlockSpec(memory_space=pltpu.VMEM)
    tile = (8, LANES)
    out1, out2 = pl.pallas_call(
        functools.partial(kernel, (nx, ny, nz, ka, kb, kq)),
        out_shape=(jax.ShapeDtypeStruct((2, 2), F32), jax.ShapeDtypeStruct((1, 2), F32)),
        in_specs=[pl.BlockSpec(memory_space=pl.ANY)] * 6,
        out_specs=(vmem, vmem),
        scratch_shapes=[
            pltpu.VMEM((2, 2, width), jnp.bfloat16),
            pltpu.VMEM((tiles, LANES), jnp.bfloat16),
            pltpu.SMEM((2, 2), jnp.int32),
            pltpu.SMEM((2,), jnp.int32),
            pltpu.SMEM((2,), jnp.int32),
            pltpu.VMEM((width, 2 * voc), jnp.bfloat16),
            pltpu.VMEM((ny, nz, ka + 1 + kq, rows, LANES), jnp.bfloat16),
            pltpu.VMEM((ny, nz, kb, rows, LANES), jnp.bfloat16),
            pltpu.VMEM((3, ny, nz, kq, rows, LANES), jnp.bfloat16),
            pltpu.VMEM((nx, kq, rows, LANES), jnp.bfloat16),
            pltpu.VMEM((ny, nz, rows, 2 * voc), F32),
            pltpu.VMEM((nz, ny, rows, LANES), F32),
            pltpu.VMEM((nx, 2, 2, width), jnp.bfloat16),
            pltpu.VMEM((nx,) + tile, F32),
            pltpu.VMEM(tile, F32),
            pltpu.VMEM((nz - 1,) + tile, F32),
            pltpu.VMEM((nz - 1,) + tile, F32),
            pltpu.VMEM((ny - 1,) + tile, F32),
            pltpu.VMEM((nx - 1,) + tile, F32),
            pltpu.VMEM(tile, F32),
            pltpu.VMEM(tile, F32),
            pltpu.VMEM(tile, F32),
            pltpu.VMEM(tile, F32),
            dma((6,)), dma, dma,
            dma((nx - 1,)), dma((nx - 1,)), dma((nx - 1,)), dma((nx - 1,)),
            dma, dma,
            dma((count_a,)), dma((count_a,)), dma((count_b,)), dma((count_b,)),
            dma, dma((3 * ny * nz,)),
            dma((nz - 1,)), dma((nz - 1,)), dma((ny - 1,)), dma((ny - 1,)), dma((nx - 1,)), dma((nx - 1,)),
        ],
        compiler_params=pltpu.CompilerParams(collective_id=0, has_side_effects=True),
        name="gather_score",
    )(hidden, lm_head, reward_head.reshape(tiles, LANES), target_ids, lengths, prompt_ids)
    return out1, out2.reshape(2)


def solution(mesh):
    split = Mesh(mesh.devices.reshape(mesh.shape["rep"], 8, 4, 2), REP_DP)
    placed = (P(REP_DP, None, None), P(None, REP_DP), P(), P(REP_DP, None), P(REP_DP), P(REP_DP))
    return jax.shard_map(
        local, mesh=split, in_specs=placed, out_specs=(P(REP_DP, None), P(REP_DP)), check_vma=False
    )
```

time: 90.2 us -> 82.7 us (0.917)
  Pallas kernels: 85.6 us -> 79.5 us
  local copies, waits for them, and re-layouts: 3.7 us -> 2.36 us
    pallas_call x1, Pallas kernels: 85.6 us -> 79.5 us  [local(): pl.pallas_call(functools.partial(kernel, (nx, ny, nz, ka, kb, kq)), out_s...]
    reshape x1 -> x0, local copies, waits for them, and re-layouts: 1.31 us -> none  [local(): reward_head.reshape(1, width)]
where the time goes in v2:
time: 82.7 us; the launch traced here: 82.5 us
  Pallas kernels  79.5 us (96%)
  local copies, waits for them, and re-layouts  2.36 us (3%)
    pallas_call x1, Pallas kernels, local(): pl.pallas_call(functools.partial(kernel, (nx, ny, nz, ka, kb, kq)), out_s...  79.5 us
    unnamed x2, local copies, waits for them, and re-layouts  2.36 us

profile of v2, /device:TPU:8, one launch (start us, length us, event | category | flops | bytes accessed | tf_op | source)
XLA Modules:
  0.0 82.5 jit_solution(18187607835862147774)
XLA Ops:
  0.6 79.5 %gather_score.1 = (f32[2,2]{1,0:T(2,128)}, f32[1,2]{1,0:T(1,128)}) custom-call(bf16[2,2,3584]{2,1,0:T(2,128)(2,1)} %hid_in.1, bf16[3584,384]{1,0:T(8,128)(2,1)} %whbm.1, bf16[28,128]{1,0:T(8,128)(2,1)} %bitcast.2, s32[2,2]{1,0:T(2,128)} %ids_in.1, s32[2]{0:T(128)} %lens_in.1, s32[2]{0:T(128)} %pids_in.1), custom_call_target="tpu_custom_call" | custom-call | tf_op jit(solution)/shard_map/gather_score/pallas_call | solution.py:408
  80.2 1.2 %copy.10 = f32[2,2]{1,0:T(2,128)} copy(f32[2,2]{1,0:T(2,128)} %get-tuple-element.8) | data formatting | bytes 32
  81.4 1.1 %copy.11 = f32[2]{0:T(128)} copy(f32[2]{0:T(128)} %bitcast.3) | data formatting | bytes 16

commit v3 on v2

--- a/solution.py
+++ b/solution.py
@@ -61,7 +61,7 @@
     hid, rhead, ids, lens, pids,
     wmat, abuf, bbuf, cbuf, quarter, acc, side, gath, gmeta, meta, tiles, got_z, got_y, got_x, sum_y, sum_x, pair, pgot,
     in_sem, w_send, w_recv, g_send, g_recv, m_send, m_recv, p_send, p_recv,
-    a_send, a_recv, b_send, b_recv, c_send, c_recv, z_send, z_recv, y_send, y_recv, x_send, x_recv,
+    a_send, a_recv, b_send, b_recv, c_send, c_recv, d_recv, z_send, z_recv, y_send, y_recv, x_send, x_recv,
 ):
     nx, ny, nz, ka, kb, kq = sizes
     rows = nx * 4
@@ -113,10 +113,13 @@
     def take(ref, sem):
         pltpu.make_async_copy(ref, ref, sem).wait()
 
+    def take_tiles(n, sem):
+        take(bbuf.at[pl.ds(0, n)], sem)
+
     for d in range(1, nx):
         send(hid, gath.at[x], g_send.at[d - 1], g_recv.at[d - 1], {AXX: at(x, d, nx)})
     for d in range(1, nx):
-        send(meta, gmeta.at[x], m_send.at[d - 1], m_recv.at[d - 1], {AXX: at(x, d, nx)})
+        send(meta, gmeta.at[x], m_send, m_recv.at[d - 1], {AXX: at(x, d, nx)}, keep=False)
     send(whbm, wmat.at[:, pl.ds(voc, voc)], w_send, w_recv, {AXC: 1 - c})
 
     gath[x] = hid[...]
@@ -150,13 +153,14 @@
     pieces = [whole[:, k * LANES:(k + 1) * LANES] for k in range(ka + kb + nx * kq)]
     for k in range(nx * kq):
         quarter[k // kq, k % kq] = pieces[ka + kb + k]
+    base_a, base_b = (y * nz + z) * (ka + 1 + kq), (y * nz + z) * kb
     for k in range(ka):
-        abuf[y, z, k] = pieces[k]
+        abuf[base_a + k] = pieces[k]
     for k in range(kb):
-        bbuf[y, z, k] = pieces[ka + k]
-    abuf[y, z, ka] = jnp.concatenate([gmeta[i, 0:4] for i in range(nx)], axis=0).astype(jnp.bfloat16)
+        bbuf[base_b + k] = pieces[ka + k]
+    abuf[base_a + ka] = jnp.concatenate([gmeta[i, 0:4] for i in range(nx)], axis=0).astype(jnp.bfloat16)
     for k in range(kq):
-        abuf[y, z, ka + 1 + k] = quarter[x, k]
+        abuf[base_a + ka + 1 + k] = quarter[x, k]
 
     send(pair, pgot, p_send, p_recv, {AXC: 1 - c})
 
@@ -165,24 +169,43 @@
     place = {(dy % ny, dz % nz): i for i, (dy, dz) in enumerate(groups)}
     far_of = [hops(ny, dy) + hops(nz, dz) for dy, dz in groups]
     where = [(at(y, dy, ny), at(z, dz, nz)) for dy, dz in groups]
+    flat = [qy * nz + qz for qy, qz in where]
+
+    def in_a(i, k=0):
+        return flat[i] * (ka + 1 + kq) + k
+
+    def in_b(i, k=0):
+        return flat[i] * kb + k
+
+    def in_c(r, i, k=0):
+        return (r * many + flat[i]) * kq + k
+
+    def block_c(r, i):
+        return cbuf.at[pl.ds(in_c(r, i), kq)]
+
+    wave_of = [[i for i in range(many) if far_of[i] == w] for w in range(ny // 2 + nz // 2 + 1)]
+
+    chunks = [sum(wave_of[:3], [])] + wave_of[3:-2] + [sum(wave_of[-2:], [])]
+    part_of = {i: n for n, chunk in enumerate(chunks) for i in chunk}
 
     def spread(i):
         for n, way in enumerate((1, -1)):
             send(
-                abuf.at[where[i] + (pl.ds(ka + 1, kq),)], cbuf.at[(n,) + where[i]],
-                c_send, c_recv.at[n * many + i], {AXX: at(x, way, nx)}, keep=False,
+                abuf.at[pl.ds(in_a(i, ka + 1), kq)], block_c(n, i),
+                c_send, c_recv.at[2 * far_of[i] + n], {AXX: at(x, way, nx)}, keep=False,
             )
 
-    def spread_on(i):
+    def spread_on(wave):
         for n in range(2):
-            take(cbuf.at[(n,) + where[i]], c_recv.at[n * many + i])
-        n = i % 2
-        send(
-            cbuf.at[(n,) + where[i]], cbuf.at[(2,) + where[i]],
-            c_send, c_recv.at[2 * many + i], {AXX: at(x, 1 - 2 * n, nx)}, keep=False,
-        )
-
-    def colour(buf, first, p1, n1, axis1, p2, n2, axis2, ssem, rsem):
+            take_tiles(len(wave_of[wave]) * kq, c_recv.at[2 * wave + n])
+        for i in wave_of[wave]:
+            n = i % 2
+            send(
+                block_c(n, i), block_c(2, i),
+                c_send, d_recv.at[part_of[i]], {AXX: at(x, 1 - 2 * n, nx)}, keep=False,
+            )
+
+    def colour(first, p1, n1, axis1, p2, n2, axis2, ssem, rsem):
         offs = ring_offsets(n1)
         ev1, ev2 = first_events(n1), second_events(n1, n2)
         index1 = {e: i for i, e in enumerate(ev1)}
@@ -190,19 +213,19 @@
 
         def block(off1, off2):
             i = place[(off1 % n1, off2 % n2) if first else (off2 % n2, off1 % n1)]
-            return i, buf.at[where[i]]
+            return i, (abuf.at[pl.ds(in_a(i), ka + 1 + kq)] if first else bbuf.at[pl.ds(in_b(i), kb)])
 
         def put1(d, way):
             if (d, way) in index1:
                 i = index1[(d, way)]
                 b = block(-way * (d - 1), 0)[1]
-                send(b, b, ssem.at[i], rsem.at[i], {axis1: at(p1, way, n1)})
+                send(b, b, ssem, rsem.at[i], {axis1: at(p1, way, n1)}, keep=False)
 
         def put2(j, d, way):
             if (j, d, way) in index2:
                 i = index2[(j, d, way)]
                 b = block(offs[j], -way * (d - 1))[1]
-                send(b, b, ssem.at[i], rsem.at[i], {axis2: at(p2, way, n2)})
+                send(b, b, ssem, rsem.at[i], {axis2: at(p2, way, n2)}, keep=False)
 
         def begin():
             for way in (1, -1):
@@ -236,8 +259,8 @@
         ]
         return begin, events
 
-    begin_a, events_a = colour(abuf, True, y, ny, AXY, z, nz, AXZ, a_send, a_recv)
-    begin_b, events_b = colour(bbuf, False, z, nz, AXZ, y, ny, AXY, b_send, b_recv)
+    begin_a, events_a = colour(True, y, ny, AXY, z, nz, AXZ, a_send, a_recv)
+    begin_b, events_b = colour(False, z, nz, AXZ, y, ny, AXY, b_send, b_recv)
     begin_a()
     begin_b()
 
@@ -252,11 +275,11 @@
             left = []
             for i in chunk:
                 if last:
-                    parts = [abuf[where[i] + (ka + 1 + k,)] for k in range(kq)]
-                    parts += [cbuf[(r,) + where[i] + (k,)] for r in range(3) for k in range(kq)]
+                    parts = [abuf[in_a(i, ka + 1 + k)] for k in range(kq)]
+                    parts += [cbuf[in_c(r, i, k)] for r in range(3) for k in range(kq)]
                 else:
-                    parts = [abuf[where[i] + (k,)] for k in range(ka)]
-                    parts += [bbuf[where[i] + (k,)] for k in range(kb)]
+                    parts = [abuf[in_a(i, k)] for k in range(ka)]
+                    parts += [bbuf[in_b(i, k)] for k in range(kb)]
                 left.append(jnp.concatenate(parts, axis=1))
             left = jnp.concatenate(left, axis=0)
             if last:
@@ -284,17 +307,14 @@
         lane_t = lax.broadcasted_iota(jnp.int32, (toks, LANES), 1)
         peak = jnp.max(logits(), axis=1, keepdims=True)
         total = jnp.sum(jnp.exp(logits() - peak), axis=1, keepdims=True)
-        dig = jnp.concatenate([abuf[where[i] + (ka,)] for i in chunk], axis=0).astype(F32)
+        dig = jnp.concatenate([abuf[in_a(i, ka)] for i in chunk], axis=0).astype(F32)
         want = (dig[:, 0:1] * 65536.0 + dig[:, 1:2] * 256.0 + dig[:, 2:3]).astype(jnp.int32)
         picked = jnp.sum(jnp.where(entry == want, logits(), 0.0), axis=1, keepdims=True)
         out = jnp.where(lane_t == 0, peak, jnp.where(lane_t == 1, total, jnp.where(lane_t == 2, picked, 0.0)))
         for m, i in enumerate(chunk):
             side[where[i][1], where[i][0]] = out[m * rows:(m + 1) * rows]
 
-    cuts = [0, many // 4, many // 2, 3 * many // 4, 7 * many // 8, many]
-    chunks = [list(range(s, e)) for s, e in zip(cuts[:-1], cuts[1:])]
-    whole_part, last_part = list(chunks), list(chunks)
-    spread_wait = list(range(many))
+    whole_part, last_part = list(chunks), list(enumerate(chunks))
     waves = ny // 2 + nz // 2
     ready = False
     for wave in range(1, waves + 3):
@@ -304,19 +324,17 @@
                 for m in mine:
                     if n < len(m):
                         m[n][2]()
-        for i in [i for i in spread_wait if far_of[i] < wave]:
-            spread_on(i)
-            spread_wait.remove(i)
+        if wave - 1 <= waves:
+            spread_on(wave - 1)
         while whole_part and max(far_of[i] for i in whole_part[0]) <= wave:
             if not ready:
                 loads[5].wait()
                 take(wmat.at[:, pl.ds(voc, voc)], w_recv)
                 ready = True
             product(whole_part.pop(0), False)
-        while last_part and max(far_of[i] for i in last_part[0]) <= wave - 2:
-            chunk = last_part.pop(0)
-            for i in chunk:
-                take(cbuf.at[(2,) + where[i]], c_recv.at[2 * many + i])
+        while last_part and max(far_of[i] for i in last_part[0][1]) <= wave - 2:
+            part, chunk = last_part.pop(0)
+            take_tiles(len(chunk) * kq, d_recv.at[part])
             product(chunk, True)
             score(chunk)
 
@@ -335,7 +353,7 @@
         q = lax.rem(z + d, nz)
         tiles[i] = slab(q)
         pltpu.make_async_remote_copy(
-            src_ref=tiles.at[i], dst_ref=got_z.at[i], send_sem=z_send.at[i], recv_sem=z_recv.at[i],
+            src_ref=tiles.at[i], dst_ref=got_z.at[i], send_sem=z_send, recv_sem=z_recv.at[i],
             device_id={AXZ: q}, device_id_type=MESH,
         ).start()
         return carry
@@ -353,13 +371,13 @@
     sum_y[...] = merge([mine] + [got_z[i] for i in range(nz - 1)])
     far = sorted(range(1, ny), key=lambda d: -hops(ny, d))
     for d in far:
-        send(sum_y, got_y.at[d - 1], y_send.at[d - 1], y_recv.at[d - 1], {AXY: at(y, d, ny)})
+        send(sum_y, got_y.at[d - 1], y_send, y_recv.at[d - 1], {AXY: at(y, d, ny)}, keep=False)
     for d in reversed(far):
         pltpu.make_async_copy(got_y.at[d - 1], got_y.at[d - 1], y_recv.at[d - 1]).wait()
     sum_x[...] = merge([sum_y[...]] + [got_y[d - 1] for d in range(1, ny)])
     far = sorted(range(1, nx), key=lambda d: -hops(nx, d))
     for d in far:
-        send(sum_x, got_x.at[d - 1], x_send.at[d - 1], x_recv.at[d - 1], {AXX: at(x, d, nx)})
+        send(sum_x, got_x.at[d - 1], x_send, x_recv.at[d - 1], {AXX: at(x, d, nx)}, keep=False)
     for d in reversed(far):
         pltpu.make_async_copy(got_x.at[d - 1], got_x.at[d - 1], x_recv.at[d - 1]).wait()
     done = merge([sum_x[...]] + [got_x[d - 1] for d in range(1, nx)])
@@ -387,9 +405,11 @@
 
     for copy in started:
         copy.wait_send()
-    take(cbuf, c_send)
-    for i in range(nz - 1):
-        pltpu.make_async_copy(tiles.at[i], tiles.at[i], z_send.at[i]).wait()
+    take_tiles((many - 1) * (ka + 1 + kq), a_send)
+    take_tiles((many - 1) * kb, b_send)
+    take_tiles(3 * many * kq, c_send)
+    for n, sem in ((nz - 1, z_send), (ny - 1, y_send), (nx - 1, x_send), (nx - 1, m_send)):
+        take_tiles(n, sem)
 
 
 def local(hidden, lm_head, reward_head, target_ids, lengths, prompt_ids):
@@ -417,9 +437,9 @@
             pltpu.SMEM((2,), jnp.int32),
             pltpu.SMEM((2,), jnp.int32),
             pltpu.VMEM((width, 2 * voc), jnp.bfloat16),
-            pltpu.VMEM((ny, nz, ka + 1 + kq, rows, LANES), jnp.bfloat16),
-            pltpu.VMEM((ny, nz, kb, rows, LANES), jnp.bfloat16),
-            pltpu.VMEM((3, ny, nz, kq, rows, LANES), jnp.bfloat16),
+            pltpu.VMEM((ny * nz * (ka + 1 + kq), rows, LANES), jnp.bfloat16),
+            pltpu.VMEM((ny * nz * kb, rows, LANES), jnp.bfloat16),
+            pltpu.VMEM((3 * ny * nz * kq, rows, LANES), jnp.bfloat16),
             pltpu.VMEM((nx, kq, rows, LANES), jnp.bfloat16),
             pltpu.VMEM((ny, nz, rows, 2 * voc), F32),
             pltpu.VMEM((nz, ny, rows, LANES), F32),
@@ -435,11 +455,11 @@
             pltpu.VMEM(tile, F32),
             pltpu.VMEM(tile, F32),
             dma((6,)), dma, dma,
-            dma((nx - 1,)), dma((nx - 1,)), dma((nx - 1,)), dma((nx - 1,)),
+            dma((nx - 1,)), dma((nx - 1,)), dma, dma((nx - 1,)),
             dma, dma,
-            dma((count_a,)), dma((count_a,)), dma((count_b,)), dma((count_b,)),
-            dma, dma((3 * ny * nz,)),
-            dma((nz - 1,)), dma((nz - 1,)), dma((ny - 1,)), dma((ny - 1,)), dma((nx - 1,)), dma((nx - 1,)),
+            dma, dma((count_a,)), dma, dma((count_b,)),
+            dma, dma((ny + nz + 2,)), dma((ny // 2 + nz // 2 - 2,)),
+            dma, dma((nz - 1,)), dma, dma((ny - 1,)), dma, dma((nx - 1,)),
         ],
         compiler_params=pltpu.CompilerParams(collective_id=0, has_side_effects=True),
         name="gather_score",

time: 82.7 us -> 80.9 us (0.978)
  the two profiles are of different devices: /device:TPU:8 before, /device:TPU:2 now
where the time goes in v3:
time: 80.9 us; the launch traced here: 80.7 us
  Pallas kernels  77.7 us (96%)
  local copies, waits for them, and re-layouts  2.36 us (3%)
    pallas_call x1, Pallas kernels, local(): pl.pallas_call(functools.partial(kernel, (nx, ny, nz, ka, kb, kq)), out_s...  77.7 us
    unnamed x2, local copies, waits for them, and re-layouts  2.36 us

profile of v3, /device:TPU:2, one launch (start us, length us, event | category | flops | bytes accessed | tf_op | source)
XLA Modules:
  0.0 80.7 jit_solution(14146482524310937266)
XLA Ops:
  0.6 77.7 %gather_score.1 = (f32[2,2]{1,0:T(2,128)}, f32[1,2]{1,0:T(1,128)}) custom-call(bf16[2,2,3584]{2,1,0:T(2,128)(2,1)} %hid_in.1, bf16[3584,384]{1,0:T(8,128)(2,1)} %whbm.1, bf16[28,128]{1,0:T(8,128)(2,1)} %bitcast.2, s32[2,2]{1,0:T(2,128)} %ids_in.1, s32[2]{0:T(128)} %lens_in.1, s32[2]{0:T(128)} %pids_in.1), custom_call_target="tpu_custom_call" | custom-call | tf_op jit(solution)/shard_map/gather_score/pallas_call | solution.py:428
  78.3 1.2 %copy.10 = f32[2,2]{1,0:T(2,128)} copy(f32[2,2]{1,0:T(2,128)} %get-tuple-element.8) | data formatting | bytes 32
  79.6 1.1 %copy.11 = f32[2]{0:T(128)} copy(f32[2]{0:T(128)} %bitcast.3) | data formatting | bytes 16

commit v4 on v3

v4 whole, which is shorter than its diff:
```python
import functools

import jax
import jax.numpy as jnp
from jax import lax
from jax.experimental import pallas as pl
from jax.experimental.pallas import tpu as pltpu
from jax.sharding import Mesh
from jax.sharding import PartitionSpec as P

GROUP = 16
PROMPTS = 64
REP_DP = ("rep", "dp_0", "dp_1", "dp_2")
AXY, AXZ, AXX, AXC = REP_DP
LANES = 128
MESH = pl.DeviceIdType.MESH
F32 = jnp.float32


def ring_offsets(n):
    order = [0]
    for d in range(1, n // 2 + 1):
        order.append(-d)
        if 2 * d < n:
            order.append(d)
    return order


def hops(n, off):
    return min(off % n, -off % n)


def plan(ny, nz, sizes, depth=1.5, rate=46.6e3, lag=2.2, least=8, most=16):
    parts = {"a": (0, ny, nz), "b": (1, nz, ny), "c": (0, ny, nz)}
    groups = [(dy % ny, dz % nz) for dy in ring_offsets(ny) for dz in ring_offsets(nz)]
    now, free, pending, issued, arrive = [0.0], {}, {}, {}, {}
    ops = []
    extra = {"a": 0, "b": 0, "c": 2}

    def queue(link, left, colour, event, what):
        pending.setdefault(link, []).append((-left, len(ops), colour, event, what))

    def issue():
        for link, wait in sorted(pending.items()):
            while wait and free.get(link, 0.0) - now[0] < depth:
                wait.sort(key=lambda w: w[0])
                left, _, colour, event, what = wait.pop(0)
                start = max(now[0], free.get(link, 0.0))
                free[link] = start + sizes[colour] / rate
                arrive[event] = max(arrive.get(event, 0.0), free[link] + lag)
                issued[event] = issued.get(event, 0) + 1
                ops.append(("send", link, event, what))

    def place(colour, off1, off2):
        swap, n1, n2 = parts[colour]
        return (off2 % n2, off1 % n1) if swap else (off1 % n1, off2 % n2)

    def ways(n, d):
        return (1, -1) if 2 * d < n else (1,)

    need, outstanding = {}, set()

    def put1(colour, d, way):
        swap, n1, n2 = parts[colour]
        if d <= n1 // 2 and way in ways(n1, d):
            event = ("p1", colour, d)
            need[event] = len(ways(n1, d))
            outstanding.add(event)
            queue(("zy" if swap else "yz")[0] + "+-"[way < 0], n1 // 2 - d + n2 // 2 + extra[colour], colour, event,
                  place(colour, -way * (d - 1), 0))

    def put2(colour, j, d, way):
        swap, n1, n2 = parts[colour]
        if d > n2 // 2:
            return
        if 2 * d == n2 and way != (1 if j % 4 in (0, 3) else -1):
            return
        event = ("p2", colour, j, d)
        need[event] = 2 if 2 * d < n2 else 1
        outstanding.add(event)
        queue(("zy" if swap else "yz")[1] + "+-"[way < 0], n2 // 2 - d + extra[colour], colour, event,
              place(colour, ring_offsets(n1)[j], -way * (d - 1)))

    have = {c: set() for c in "abc"}

    def got(colour, g):
        have[colour].add(g)
        if colour == "c":
            event = ("x1", g)
            need[event] = 2
            outstanding.add(event)
            for way in "+-":
                queue("x" + way, 1, "c", event, g)

    def take(event):
        kind = event[0]
        if kind == "x1":
            g = event[1]
            way = "+-"[groups.index(g) % 2]
            queue("x" + way, 0, "c", ("x2", g), g)
            return
        colour = event[1]
        swap, n1, n2 = parts[colour]
        if kind == "p1":
            d = event[2]
            for way in ways(n1, d):
                put1(colour, d + 1, way)
                j = [o % n1 for o in ring_offsets(n1)].index(-way * d % n1)
                for w2 in (1, -1):
                    put2(colour, j, 1, w2)
                got(colour, place(colour, -way * d, 0))
        else:
            j, d = event[2:]
            for way in (1, -1) if 2 * d < n2 else ((1 if j % 4 in (0, 3) else -1),):
                put2(colour, j, d + 1, way)
                got(colour, place(colour, ring_offsets(n1)[j], -way * d))

    for colour in "cab":
        for way in (1, -1):
            put1(colour, 1, way)
        for way in (1, -1):
            put2(colour, 0, 1, way)
        got(colour, (0, 0))
    first_done, last_done = [], []
    while len(last_done) < len(groups):
        issue()
        ready = [e for e in outstanding if issued.get(e, 0) == need[e]]
        ready.sort(key=lambda e: (arrive[e], str(e)))
        if ready and arrive[ready[0]] <= now[0]:
            event = ready[0]
            outstanding.discard(event)
            ops.append(("take", event))
            now[0] += 0.03
            take(event)
            continue
        left = [g for g in groups if g not in first_done]
        one = [g for g in left if g in have["a"] and g in have["b"]][:most]
        todo = [g for g in groups if g not in last_done]
        two = [g for g in first_done if g not in last_done and issued.get(("x2", g)) and arrive[("x2", g)] <= now[0]][:most]
        if one and (len(one) >= least or len(one) == len(left)) and not (two and len(two) >= least):
            first_done.extend(one)
            ops.append(("first", tuple(one)))
            now[0] += 0.75 + 0.037 * len(one)
        elif two and (len(two) >= least or len(two) == len(todo)):
            last_done.extend(two)
            ops.append(("last", tuple(two)))
            now[0] += 0.9 + 0.045 * len(two)
        elif ready:
            now[0] = arrive[ready[0]]
        else:
            late = [arrive[("x2", g)] for g in todo if issued.get(("x2", g)) and arrive[("x2", g)] > now[0]]
            nxt = min(late) if late else None
            if nxt is None:
                nxt = min(free[l] for l in pending if pending[l]) - depth + 1e-6
            now[0] = max(nxt, now[0])
    return ops, need


def kernel(
    sizes, steps, need, hid_in, whbm, rhead_in, ids_in, lens_in, pids_in, out1, out2,
    hid, rhead, ids, lens, pids,
    wmat, abuf, bbuf, own, cbuf, quarter, acc, side, gath, gmeta, meta, tiles, got_z, got_y, got_x, sum_y, sum_x, pair, pgot,
    in_sem, w_send, w_recv, g_send, g_recv, m_send, m_recv, p_send, p_recv,
    a_send, b_send, c_send, o_send, e_recv, d_recv, z_send, z_recv, y_send, y_recv, x_send, x_recv,
):
    nx, ny, nz, ka, kb, kq = sizes
    rows = nx * 4
    voc = whbm.shape[1]
    y, z, x, c = (lax.axis_index(a) for a in (AXY, AXZ, AXX, AXC))

    def at(pos, off, n):
        return lax.rem(pos + (off % n), n)

    barrier = pltpu.get_barrier_semaphore()
    partners = [{AXX: at(x, d, nx)} for d in range(1, nx)]
    partners += [{AXY: at(y, d, ny)} for d in (1, -1)]
    partners += [{AXZ: at(z, d, nz)} for d in (1, -1)]
    partners += [{AXC: 1 - c}]
    for dev in partners:
        pl.semaphore_signal(barrier, inc=1, device_id=dev, device_id_type=MESH)

    loads = [
        pltpu.make_async_copy(src, dst, in_sem.at[i])
        for i, (src, dst) in enumerate((
            (hid_in, hid), (ids_in, ids), (lens_in, lens), (pids_in, pids), (rhead_in, rhead),
            (whbm, wmat.at[:, pl.ds(0, voc)]),
        ))
    ]
    for load in loads:
        load.start()
    loads[0].wait()
    loads[1].wait()

    row8 = lax.broadcasted_iota(jnp.int32, (8, LANES), 0)
    lane8 = lax.broadcasted_iota(jnp.int32, (8, LANES), 1)
    idv = jnp.zeros((8, LANES), jnp.int32)
    for t in range(4):
        idv = jnp.where(row8 == t, ids[t // 2, t % 2], idv)
    digits = jnp.where(lane8 == 0, idv >> 16, jnp.where(lane8 == 1, (idv >> 8) & 255, idv & 255))
    meta[...] = jnp.where(lane8 < 3, digits, 0).astype(F32)
    pl.semaphore_wait(barrier, len(partners))

    started = []

    def send(src, dst, ssem, rsem, dev, keep=True):
        copy = pltpu.make_async_remote_copy(
            src_ref=src, dst_ref=dst, send_sem=ssem, recv_sem=rsem, device_id=dev, device_id_type=MESH
        )
        copy.start()
        if keep:
            started.append(copy)

    def take(ref, sem):
        pltpu.make_async_copy(ref, ref, sem).wait()

    def take_tiles(n, sem):
        take(bbuf.at[pl.ds(0, n)], sem)

    for d in range(1, nx):
        send(hid, gath.at[x], g_send.at[d - 1], g_recv, {AXX: at(x, d, nx)})
    for d in range(1, nx):
        send(meta, gmeta.at[x], m_send, m_recv, {AXX: at(x, d, nx)}, keep=False)
    send(whbm, wmat.at[:, pl.ds(voc, voc)], w_send, w_recv, {AXC: 1 - c})

    gath[x] = hid[...]
    gmeta[x] = meta[...]

    for load in loads[2:5]:
        load.wait()
    rewards = []
    for r in range(2):
        both = sum(
            hid[r, :, pl.ds(k * LANES, LANES)].astype(F32) * rhead[k:k + 1].astype(F32)
            for k in range(rhead.shape[0])
        )
        both = jnp.sum(both, axis=1, keepdims=True)
        rewards.append(jnp.where(lens[r] == 1, both[0:1], both[1:2]))
    lane1 = lax.broadcasted_iota(jnp.int32, (1, LANES), 1)
    stacked = jnp.zeros((1, LANES), F32)
    for r in range(2):
        stacked += jnp.where(lane1 == pids[r], rewards[r], 0.0)
        stacked += jnp.where(lane1 == pids[r] + PROMPTS, rewards[r] * rewards[r], 0.0)
    pair[...] = jnp.where(row8 == 3, stacked, 0.0)

    take(gath.at[pl.ds(0, nx - 1)], g_recv)
    take(gmeta.at[pl.ds(0, nx - 1)], m_recv)

    whole = jnp.concatenate(
        [gath[i, r].astype(F32) for i in range(nx) for r in range(2)], axis=0
    ).astype(jnp.bfloat16)
    pieces = [whole[:, k * LANES:(k + 1) * LANES] for k in range(ka + kb + nx * kq)]
    for k in range(nx * kq):
        quarter[k // kq, k % kq] = pieces[ka + kb + k]
    base_a, base_b, base_o = (y * nz + z) * (ka + 1), (y * nz + z) * kb, (y * nz + z) * kq
    for k in range(ka):
        abuf[base_a + k] = pieces[k]
    for k in range(kb):
        bbuf[base_b + k] = pieces[ka + k]
    abuf[base_a + ka] = jnp.concatenate([gmeta[i, 0:4] for i in range(nx)], axis=0).astype(jnp.bfloat16)
    for k in range(kq):
        own[base_o + k] = quarter[x, k]

    send(pair, pgot, p_send, p_recv, {AXC: 1 - c})

    groups = [(dy % ny, dz % nz) for dy in ring_offsets(ny) for dz in ring_offsets(nz)]
    many = len(groups)
    where = {g: (at(y, g[0], ny), at(z, g[1], nz)) for g in groups}
    flat = {g: qy * nz + qz for g, (qy, qz) in where.items()}
    tiles_of = {"a": ka + 1, "b": kb, "c": kq}
    store = {"a": abuf, "b": bbuf, "c": own}
    out_sem = {"a": a_send, "b": b_send, "c": o_send}
    axis = {"x": (AXX, x, nx), "y": (AXY, y, ny), "z": (AXZ, z, nz)}
    index = {event: i for i, event in enumerate(sorted(need, key=str))}
    part_of = {g: n for n, op in enumerate([op for op in steps if op[0] == "last"]) for g in op[1]}

    def in_a(g, k=0):
        return flat[g] * (ka + 1) + k

    def in_b(g, k=0):
        return flat[g] * kb + k

    def in_c(r, g, k=0):
        return (r * many + flat[g]) * kq + k

    def block(colour, g):
        n = tiles_of[colour]
        return store[colour].at[pl.ds(flat[g] * n, n)]

    def put(link, event, g):
        name, pos, n = axis[link[0]]
        dev = {name: at(pos, 1 if link[1] == "+" else -1, n)}
        side_in = "+-".index(link[1])
        if event[0] == "x1":
            there = cbuf.at[pl.ds(in_c(side_in, g), kq)]
            send(block("c", g), there, c_send, e_recv.at[index[event]], dev, keep=False)
        elif event[0] == "x2":
            here, there = cbuf.at[pl.ds(in_c(side_in, g), kq)], cbuf.at[pl.ds(in_c(2, g), kq)]
            send(here, there, c_send, d_recv.at[part_of[g]], dev, keep=False)
        else:
            b = block(event[1], g)
            send(b, b, out_sem[event[1]], e_recv.at[index[event]], dev, keep=False)

    def get(event):
        take_tiles(need[event] * tiles_of["c" if event[0] == "x1" else event[1]], e_recv.at[index[event]])

    wide = 2 * LANES
    chip = ((y * nz + z) * nx + x) * 2
    turns = [at(x, off, nx) for off in (0, -1, 1, 2)]
    starts = [pl.multiple_of((ka + kb + q * kq) * LANES, LANES) for q in turns]

    def product(chunk, last):
        def step(n, carry):
            cols = pl.ds(pl.multiple_of(n * wide, wide), wide)
            left = []
            for i in chunk:
                if last:
                    parts = [own[flat[i] * kq + k] for k in range(kq)]
                    parts += [cbuf[in_c(r, i, k)] for r in range(3) for k in range(kq)]
                else:
                    parts = [abuf[in_a(i, k)] for k in range(ka)]
                    parts += [bbuf[in_b(i, k)] for k in range(kb)]
                left.append(jnp.concatenate(parts, axis=1))
            left = jnp.concatenate(left, axis=0)
            if last:
                right = jnp.concatenate([wmat[pl.ds(s, kq * LANES), cols] for s in starts], axis=0)
            else:
                right = wmat[pl.ds(0, (ka + kb) * LANES), cols]
            part = jnp.dot(left, right, preferred_element_type=F32)
            for m, i in enumerate(chunk):
                piece = part[m * rows:(m + 1) * rows]
                if last:
                    piece = acc[where[i] + (slice(None), cols)] + piece
                acc[where[i] + (slice(None), cols)] = piece
            return carry

        lax.fori_loop(0, 2 * voc // wide, step, 0)

    def score(chunk):
        toks = len(chunk) * rows

        def logits():
            return jnp.concatenate([acc[where[i]] for i in chunk], axis=0)

        lane = lax.broadcasted_iota(jnp.int32, (toks, 2 * voc), 1)
        entry = jnp.where(lane < voc, (chip + c) * voc + lane, (chip + 1 - c) * voc + lane - voc)
        lane_t = lax.broadcasted_iota(jnp.int32, (toks, LANES), 1)
        peak = jnp.max(logits(), axis=1, keepdims=True)
        total = jnp.sum(jnp.exp(logits() - peak), axis=1, keepdims=True)
        dig = jnp.concatenate([abuf[in_a(i, ka)] for i in chunk], axis=0).astype(F32)
        want = (dig[:, 0:1] * 65536.0 + dig[:, 1:2] * 256.0 + dig[:, 2:3]).astype(jnp.int32)
        picked = jnp.sum(jnp.where(entry == want, logits(), 0.0), axis=1, keepdims=True)
        out = jnp.where(lane_t == 0, peak, jnp.where(lane_t == 1, total, jnp.where(lane_t == 2, picked, 0.0)))
        for m, i in enumerate(chunk):
            side[where[i][1], where[i][0]] = out[m * rows:(m + 1) * rows]

    ready = False
    count = 0
    for op in steps:
        if op[0] == "send":
            put(*op[1:])
        elif op[0] == "take":
            get(op[1])
        elif op[0] == "first":
            if not ready:
                loads[5].wait()
                take(wmat.at[:, pl.ds(voc, voc)], w_recv)
                ready = True
            product(op[1], False)
            count += 1
        else:
            take_tiles(len(op[1]) * kq, d_recv.at[part_of[op[1][0]]])
            product(op[1], True)
            score(op[1])
            count += 1

    take(pgot, p_recv)
    prompt_row = pair[...] + pgot[...]

    def slab(q):
        block = side[q].reshape(ny * rows, LANES)
        if ny * rows < LANES:
            block = jnp.concatenate([block, jnp.zeros((LANES - ny * rows, LANES), F32)], axis=0)
        return jnp.where(row8 == 3, prompt_row, block.T[0:8, :])

    def step(i, carry):
        h = (i + 1) // 2
        d = nz // 2 + h * (1 - 2 * (i % 2))
        q = lax.rem(z + d, nz)
        tiles[i] = slab(q)
        pltpu.make_async_remote_copy(
            src_ref=tiles.at[i], dst_ref=got_z.at[i], send_sem=z_send, recv_sem=z_recv,
            device_id={AXZ: q}, device_id_type=MESH,
        ).start()
        return carry

    lax.fori_loop(0, nz - 1, step, 0)

    def merge(parts):
        top = functools.reduce(jnp.maximum, [p[0:1] for p in parts])
        out = sum(p * jnp.where(row8 == 1, jnp.exp(p[0:1] - top), 1.0) for p in parts)
        return jnp.where(row8 == 0, top, out)

    mine = slab(z)
    take(got_z, z_recv)
    sum_y[...] = merge([mine] + [got_z[i] for i in range(nz - 1)])
    far = sorted(range(1, ny), key=lambda d: -hops(ny, d))
    for d in far:
        send(sum_y, got_y.at[d - 1], y_send, y_recv, {AXY: at(y, d, ny)}, keep=False)
    take(got_y, y_recv)
    sum_x[...] = merge([sum_y[...]] + [got_y[d - 1] for d in range(1, ny)])
    far = sorted(range(1, nx), key=lambda d: -hops(nx, d))
    for d in far:
        send(sum_x, got_x.at[d - 1], x_send, x_recv, {AXX: at(x, d, nx)}, keep=False)
    take(got_x, x_recv)
    done = merge([sum_x[...]] + [got_x[d - 1] for d in range(1, nx)])

    logprob = done[2:3] - (done[0:1] + jnp.log(done[1:2]))
    base = y * rows + x * 4
    r_out = lax.broadcasted_iota(jnp.int32, (2, 2), 0)
    w_out = lax.broadcasted_iota(jnp.int32, (2, 2), 1)
    value = jnp.zeros((2, 2), F32)
    for t in range(4):
        r, w = t // 2, t % 2
        one = jnp.sum(jnp.where(lane1 == base + t, logprob, 0.0), axis=1, keepdims=True)
        one = jnp.where(w < lens[r], one, 0.0)
        value = jnp.where((r_out == r) & (w_out == w), one, value)
    out1[...] = value
    moment = done[3:4] * (1.0 / GROUP)
    spot = lax.broadcasted_iota(jnp.int32, (1, 2), 1)
    adv = jnp.zeros((1, 2), F32)
    for r in range(2):
        mean = jnp.sum(jnp.where(lane1 == pids[r], moment, 0.0), axis=1, keepdims=True)
        square = jnp.sum(jnp.where(lane1 == pids[r] + PROMPTS, moment, 0.0), axis=1, keepdims=True)
        scale = jnp.sqrt(jnp.maximum(square - mean * mean, 1.0))
        adv = jnp.where(spot == r, (rewards[r] - mean) / scale, adv)
    out2[...] = adv

    for copy in started:
        copy.wait_send()
    take_tiles((many - 1) * (ka + 1), a_send)
    take_tiles((many - 1) * kq, o_send)
    take_tiles((many - 1) * kb, b_send)
    take(cbuf, c_send)
    for n, sem in ((nz - 1, z_send), (ny - 1, y_send), (nx - 1, x_send), (nx - 1, m_send)):
        take_tiles(n, sem)


def local(hidden, lm_head, reward_head, target_ids, lengths, prompt_ids):
    nx, ny, nz = (lax.axis_size(a) for a in (AXX, AXY, AXZ))
    width, voc = lm_head.shape
    tiles = width // LANES
    kq = max(1, tiles * 3 // (7 * nx))
    ka = (tiles - kq * nx) * 3 // 8
    kb = tiles - kq * nx - ka
    rows = nx * 4
    size = rows * LANES * 2
    steps, need = plan(ny, nz, {"a": (ka + 1) * size, "b": kb * size, "c": kq * size})
    lasts = sum(op[0] == "last" for op in steps)
    dma = pltpu.SemaphoreType.DMA
    vmem = pl.BlockSpec(memory_space=pltpu.VMEM)
    tile = (8, LANES)
    out1, out2 = pl.pallas_call(
        functools.partial(kernel, (nx, ny, nz, ka, kb, kq), steps, need),
        out_shape=(jax.ShapeDtypeStruct((2, 2), F32), jax.ShapeDtypeStruct((1, 2), F32)),
        in_specs=[pl.BlockSpec(memory_space=pl.ANY)] * 6,
        out_specs=(vmem, vmem),
        scratch_shapes=[
            pltpu.VMEM((2, 2, width), jnp.bfloat16),
            pltpu.VMEM((tiles, LANES), jnp.bfloat16),
            pltpu.SMEM((2, 2), jnp.int32),
            pltpu.SMEM((2,), jnp.int32),
            pltpu.SMEM((2,), jnp.int32),
            pltpu.VMEM((width, 2 * voc), jnp.bfloat16),
            pltpu.VMEM((ny * nz * (ka + 1), rows, LANES), jnp.bfloat16),
            pltpu.VMEM((ny * nz * kb, rows, LANES), jnp.bfloat16),
            pltpu.VMEM((ny * nz * kq, rows, LANES), jnp.bfloat16),
            pltpu.VMEM((3 * ny * nz * kq, rows, LANES), jnp.bfloat16),
            pltpu.VMEM((nx, kq, rows, LANES), jnp.bfloat16),
            pltpu.VMEM((ny, nz, rows, 2 * voc), F32),
            pltpu.VMEM((nz, ny, rows, LANES), F32),
            pltpu.VMEM((nx, 2, 2, width), jnp.bfloat16),
            pltpu.VMEM((nx,) + tile, F32),
            pltpu.VMEM(tile, F32),
            pltpu.VMEM((nz - 1,) + tile, F32),
            pltpu.VMEM((nz - 1,) + tile, F32),
            pltpu.VMEM((ny - 1,) + tile, F32),
            pltpu.VMEM((nx - 1,) + tile, F32),
            pltpu.VMEM(tile, F32),
            pltpu.VMEM(tile, F32),
            pltpu.VMEM(tile, F32),
            pltpu.VMEM(tile, F32),
            dma((6,)), dma, dma,
            dma((nx - 1,)), dma, dma, dma,
            dma, dma,
            dma, dma, dma, dma, dma((len(need),)), dma((lasts,)),
            dma, dma, dma, dma, dma, dma,
        ],
        compiler_params=pltpu.CompilerParams(collective_id=0, has_side_effects=True),
        name="gather_score",
    )(hidden, lm_head, reward_head.reshape(tiles, LANES), target_ids, lengths, prompt_ids)
    return out1, out2.reshape(2)


def solution(mesh):
    split = Mesh(mesh.devices.reshape(mesh.shape["rep"], 8, 4, 2), REP_DP)
    placed = (P(REP_DP, None, None), P(None, REP_DP), P(), P(REP_DP, None), P(REP_DP), P(REP_DP))
    return jax.shard_map(
        local, mesh=split, in_specs=placed, out_specs=(P(REP_DP, None), P(REP_DP)), check_vma=False
    )
```

time: 80.9 us -> 76.5 us (0.946)
  Pallas kernels: 77.7 us -> 73.4 us
    pallas_call x1, Pallas kernels: 77.7 us -> 73.4 us  [local(): pl.pallas_call(functools.partial(kernel, (nx, ny, nz, ka, kb, kq), steps,...]
where the time goes in v4:
time: 76.5 us; the launch traced here: 76.4 us
  Pallas kernels  73.4 us (96%)
  local copies, waits for them, and re-layouts  2.36 us (3%)
    pallas_call x1, Pallas kernels, local(): pl.pallas_call(functools.partial(kernel, (nx, ny, nz, ka, kb, kq), steps,...  73.4 us
    unnamed x2, local copies, waits for them, and re-layouts  2.36 us

profile of v4, /device:TPU:2, one launch (start us, length us, event | category | flops | bytes accessed | tf_op | source)
XLA Modules:
  0.0 76.4 jit_solution(6693037555826314423)
XLA Ops:
  0.6 73.4 %gather_score.1 = (f32[2,2]{1,0:T(2,128)}, f32[1,2]{1,0:T(1,128)}) custom-call(bf16[2,2,3584]{2,1,0:T(2,128)(2,1)} %hid_in.1, bf16[3584,384]{1,0:T(8,128)(2,1)} %whbm.1, bf16[28,128]{1,0:T(8,128)(2,1)} %bitcast.2, s32[2,2]{1,0:T(2,128)} %ids_in.1, s32[2]{0:T(128)} %lens_in.1, s32[2]{0:T(128)} %pids_in.1), custom_call_target="tpu_custom_call" | custom-call | tf_op jit(solution)/shard_map/gather_score/pallas_call | solution.py:462
  74.0 1.2 %copy.10 = f32[2,2]{1,0:T(2,128)} copy(f32[2,2]{1,0:T(2,128)} %get-tuple-element.8) | data formatting | bytes 32
  75.2 1.1 %copy.11 = f32[2]{0:T(128)} copy(f32[2]{0:T(128)} %bitcast.3) | data formatting | bytes 16

commit v5 on v4

--- a/solution.py
+++ b/solution.py
@@ -159,9 +159,9 @@
 def kernel(
     sizes, steps, need, hid_in, whbm, rhead_in, ids_in, lens_in, pids_in, out1, out2,
     hid, rhead, ids, lens, pids,
-    wmat, abuf, bbuf, own, cbuf, quarter, acc, side, gath, gmeta, meta, tiles, got_z, got_y, got_x, sum_y, sum_x, pair, pgot,
+    wmat, abuf, bbuf, own, cbuf, quarter, acc, side, gath, gmeta, meta, tiles, got_z, got_yx, sums, pair, pgot,
     in_sem, w_send, w_recv, g_send, g_recv, m_send, m_recv, p_send, p_recv,
-    a_send, b_send, c_send, o_send, e_recv, d_recv, z_send, z_recv, y_send, y_recv, x_send, x_recv,
+    a_send, b_send, c_send, o_send, e_recv, d_recv, z_send, z_recv, y_send, y_recv,
 ):
     nx, ny, nz, ka, kb, kq = sizes
     rows = nx * 4
@@ -310,7 +310,7 @@
 
     def product(chunk, last):
         def step(n, carry):
-            cols = pl.ds(pl.multiple_of(n * wide, wide), wide)
+            cols = pl.ds(n * wide, wide)
             left = []
             for i in chunk:
                 if last:
@@ -333,7 +333,8 @@
                 acc[where[i] + (slice(None), cols)] = piece
             return carry
 
-        lax.fori_loop(0, 2 * voc // wide, step, 0)
+        for n in range(2 * voc // wide):
+            step(n, 0)
 
     def score(chunk):
         toks = len(chunk) * rows
@@ -396,23 +397,19 @@
     lax.fori_loop(0, nz - 1, step, 0)
 
     def merge(parts):
+        row8 = lax.broadcasted_iota(jnp.int32, parts[0].shape, 0)
         top = functools.reduce(jnp.maximum, [p[0:1] for p in parts])
         out = sum(p * jnp.where(row8 == 1, jnp.exp(p[0:1] - top), 1.0) for p in parts)
         return jnp.where(row8 == 0, top, out)
 
     mine = slab(z)
     take(got_z, z_recv)
-    sum_y[...] = merge([mine] + [got_z[i] for i in range(nz - 1)])
-    far = sorted(range(1, ny), key=lambda d: -hops(ny, d))
-    for d in far:
-        send(sum_y, got_y.at[d - 1], y_send, y_recv, {AXY: at(y, d, ny)}, keep=False)
-    take(got_y, y_recv)
-    sum_x[...] = merge([sum_y[...]] + [got_y[d - 1] for d in range(1, ny)])
-    far = sorted(range(1, nx), key=lambda d: -hops(nx, d))
-    for d in far:
-        send(sum_x, got_x.at[d - 1], x_send, x_recv, {AXX: at(x, d, nx)}, keep=False)
-    take(got_x, x_recv)
-    done = merge([sum_x[...]] + [got_x[d - 1] for d in range(1, nx)])
+    sums[...] = merge([mine] + [got_z[i] for i in range(nz - 1)])[0:4]
+    others = [(dy, dx) for dy in range(ny) for dx in range(nx) if dy or dx]
+    for n, (dy, dx) in sorted(enumerate(others), key=lambda o: -hops(ny, o[1][0]) - hops(nx, o[1][1])):
+        send(sums, got_yx.at[n], y_send, y_recv, {AXY: at(y, dy, ny), AXX: at(x, dx, nx)}, keep=False)
+    take(got_yx, y_recv)
+    done = merge([sums[...]] + [got_yx[n] for n in range(len(others))])
 
     logprob = done[2:3] - (done[0:1] + jnp.log(done[1:2]))
     base = y * rows + x * 4
@@ -441,8 +438,9 @@
     take_tiles((many - 1) * kq, o_send)
     take_tiles((many - 1) * kb, b_send)
     take(cbuf, c_send)
-    for n, sem in ((nz - 1, z_send), (ny - 1, y_send), (nx - 1, x_send), (nx - 1, m_send)):
-        take_tiles(n, sem)
+    take_tiles(nz - 1, z_send)
+    take_tiles(nx - 1, m_send)
+    take(got_yx, y_send)
 
 
 def local(hidden, lm_head, reward_head, target_ids, lengths, prompt_ids):
@@ -461,7 +459,7 @@
     tile = (8, LANES)
     out1, out2 = pl.pallas_call(
         functools.partial(kernel, (nx, ny, nz, ka, kb, kq), steps, need),
-        out_shape=(jax.ShapeDtypeStruct((2, 2), F32), jax.ShapeDtypeStruct((1, 2), F32)),
+        out_shape=(pltpu.VMEM((2, 2), F32), pltpu.VMEM((1, 2), F32)),
         in_specs=[pl.BlockSpec(memory_space=pl.ANY)] * 6,
         out_specs=(vmem, vmem),
         scratch_shapes=[
@@ -483,17 +481,15 @@
             pltpu.VMEM(tile, F32),
             pltpu.VMEM((nz - 1,) + tile, F32),
             pltpu.VMEM((nz - 1,) + tile, F32),
-            pltpu.VMEM((ny - 1,) + tile, F32),
-            pltpu.VMEM((nx - 1,) + tile, F32),
-            pltpu.VMEM(tile, F32),
-            pltpu.VMEM(tile, F32),
+            pltpu.VMEM((ny * nx - 1, 4, LANES), F32),
+            pltpu.VMEM((4, LANES), F32),
             pltpu.VMEM(tile, F32),
             pltpu.VMEM(tile, F32),
             dma((6,)), dma, dma,
             dma((nx - 1,)), dma, dma, dma,
             dma, dma,
             dma, dma, dma, dma, dma((len(need),)), dma((lasts,)),
-            dma, dma, dma, dma, dma, dma,
+            dma, dma, dma, dma,
         ],
         compiler_params=pltpu.CompilerParams(collective_id=0, has_side_effects=True),
         name="gather_score",

time: 76.5 us -> 71.1 us (0.929)
  Pallas kernels: 73.4 us -> 69.3 us
  local copies, waits for them, and re-layouts: 2.36 us -> 1.08 us
    pallas_call x1, Pallas kernels: 73.4 us -> 69.3 us  [local(): pl.pallas_call(functools.partial(kernel, (nx, ny, nz, ka, kb, kq), steps,...]
    unnamed x2, local copies, waits for them, and re-layouts: 2.36 us -> 1.08 us
where the time goes in v5:
time: 71.1 us; the launch traced here: 71 us
  Pallas kernels  69.3 us (97%)
  local copies, waits for them, and re-layouts  1.08 us (2%)
    pallas_call x1, Pallas kernels, local(): pl.pallas_call(functools.partial(kernel, (nx, ny, nz, ka, kb, kq), steps,...  69.3 us

profile of v5, /device:TPU:2, one launch (start us, length us, event | category | flops | bytes accessed | tf_op | source)
XLA Modules:
  0.0 71.0 jit_solution(10796319188567304301)
XLA Ops:
  0.6 69.3 %gather_score.1 = (f32[2,2]{1,0:T(2,128)S(1)}, f32[1,2]{1,0:T(1,128)S(1)}) custom-call(bf16[2,2,3584]{2,1,0:T(2,128)(2,1)} %hid_in.1, bf16[3584,384]{1,0:T(8,128)(2,1)} %whbm.1, bf16[28,128]{1,0:T(8,128)(2,1)} %bitcast.3, s32[2,2]{1,0:T(2,128)} %ids_in.1, s32[2]{0:T(128)} %lens_in.1, s32[2]{0:T(128)} %pids_in.1), custom_call_target="tpu_custom_call" | custom-call | tf_op jit(solution)/shard_map/gather_score/pallas_call | solution.py:460
  69.9 0.6 copy.10
  70.5 0.5 copy.11

commit v6 on v5

--- a/solution.py
+++ b/solution.py
@@ -30,7 +30,7 @@
     return min(off % n, -off % n)
 
 
-def plan(ny, nz, sizes, depth=1.5, rate=46.6e3, lag=2.2, least=8, most=16):
+def plan(ny, nz, sizes, depth=0.8, rate=46.6e3, lag=2.4, least=(12, 8), most=16, tail=24):
     parts = {"a": (0, ny, nz), "b": (1, nz, ny), "c": (0, ny, nz)}
     groups = [(dy % ny, dz % nz) for dy in ring_offsets(ny) for dz in ring_offsets(nz)]
     now, free, pending, issued, arrive = [0.0], {}, {}, {}, {}
@@ -50,6 +50,7 @@
                 arrive[event] = max(arrive.get(event, 0.0), free[link] + lag)
                 issued[event] = issued.get(event, 0) + 1
                 ops.append(("send", link, event, what))
+                now[0] += 0.015
 
     def place(colour, off1, off2):
         swap, n1, n2 = parts[colour]
@@ -82,22 +83,25 @@
               place(colour, ring_offsets(n1)[j], -way * (d - 1)))
 
     have = {c: set() for c in "abc"}
-
-    def got(colour, g):
-        have[colour].add(g)
+    batch, done = {}, []
+
+    def got(colour, new):
+        have[colour].update(new)
         if colour == "c":
-            event = ("x1", g)
-            need[event] = 2
+            event = ("x1",) + new[0]
+            need[event] = 2 * len(new)
+            batch[event] = new
             outstanding.add(event)
-            for way in "+-":
-                queue("x" + way, 1, "c", event, g)
+            for g in new:
+                for way in "+-":
+                    queue("x" + way, 1, "c", event, g)
 
     def take(event):
         kind = event[0]
         if kind == "x1":
-            g = event[1]
-            way = "+-"[groups.index(g) % 2]
-            queue("x" + way, 0, "c", ("x2", g), g)
+            for n, g in enumerate(batch[event]):
+                queue("x" + "+-"[(n + len(done)) % 2], 0, "c", ("x2", g), g)
+            done.append(event)
             return
         colour = event[1]
         swap, n1, n2 = parts[colour]
@@ -108,19 +112,20 @@
                 j = [o % n1 for o in ring_offsets(n1)].index(-way * d % n1)
                 for w2 in (1, -1):
                     put2(colour, j, 1, w2)
-                got(colour, place(colour, -way * d, 0))
+            got(colour, [place(colour, -way * d, 0) for way in ways(n1, d)])
         else:
             j, d = event[2:]
-            for way in (1, -1) if 2 * d < n2 else ((1 if j % 4 in (0, 3) else -1),):
+            sides = (1, -1) if 2 * d < n2 else ((1 if j % 4 in (0, 3) else -1),)
+            for way in sides:
                 put2(colour, j, d + 1, way)
-                got(colour, place(colour, ring_offsets(n1)[j], -way * d))
+            got(colour, [place(colour, ring_offsets(n1)[j], -way * d) for way in sides])
 
     for colour in "cab":
         for way in (1, -1):
             put1(colour, 1, way)
         for way in (1, -1):
             put2(colour, 0, 1, way)
-        got(colour, (0, 0))
+        got(colour, [(0, 0)])
     first_done, last_done = [], []
     while len(last_done) < len(groups):
         issue()
@@ -137,14 +142,14 @@
         one = [g for g in left if g in have["a"] and g in have["b"]][:most]
         todo = [g for g in groups if g not in last_done]
         two = [g for g in first_done if g not in last_done and issued.get(("x2", g)) and arrive[("x2", g)] <= now[0]][:most]
-        if one and (len(one) >= least or len(one) == len(left)) and not (two and len(two) >= least):
+        if one and (len(one) >= least[len(left) <= tail] or len(one) == len(left)) and not (two and len(two) >= least[len(todo) <= tail]):
             first_done.extend(one)
             ops.append(("first", tuple(one)))
-            now[0] += 0.75 + 0.037 * len(one)
-        elif two and (len(two) >= least or len(two) == len(todo)):
+            now[0] += 0.57 + 0.02 * len(one)
+        elif two and (len(two) >= least[len(todo) <= tail] or len(two) == len(todo)):
             last_done.extend(two)
             ops.append(("last", tuple(two)))
-            now[0] += 0.9 + 0.045 * len(two)
+            now[0] += 0.6 + 0.028 * len(two)
         elif ready:
             now[0] = arrive[ready[0]]
         else:
@@ -448,7 +453,7 @@
     width, voc = lm_head.shape
     tiles = width // LANES
     kq = max(1, tiles * 3 // (7 * nx))
-    ka = (tiles - kq * nx) * 3 // 8
+    ka = max(1, (tiles - kq * nx) * 5 // 16)
     kb = tiles - kq * nx - ka
     rows = nx * 4
     size = rows * LANES * 2

time: 71.1 us -> 69.4 us (0.976)
  Pallas kernels: 69.3 us -> 67.6 us
    pallas_call x1, Pallas kernels: 69.3 us -> 67.6 us  [local(): pl.pallas_call(functools.partial(kernel, (nx, ny, nz, ka, kb, kq), steps,...]
where the time goes in v6:
time: 69.4 us; the launch traced here: 69.3 us
  Pallas kernels  67.6 us (97%)
  local copies, waits for them, and re-layouts  1.08 us (2%)
    pallas_call x1, Pallas kernels, local(): pl.pallas_call(functools.partial(kernel, (nx, ny, nz, ka, kb, kq), steps,...  67.6 us

profile of v6, /device:TPU:2, one launch (start us, length us, event | category | flops | bytes accessed | tf_op | source)
XLA Modules:
  0.0 69.3 jit_solution(9927045649622881024)
XLA Ops:
  0.6 67.6 %gather_score.1 = (f32[2,2]{1,0:T(2,128)S(1)}, f32[1,2]{1,0:T(1,128)S(1)}) custom-call(bf16[2,2,3584]{2,1,0:T(2,128)(2,1)} %hid_in.1, bf16[3584,384]{1,0:T(8,128)(2,1)} %whbm.1, bf16[28,128]{1,0:T(8,128)(2,1)} %bitcast.3, s32[2,2]{1,0:T(2,128)} %ids_in.1, s32[2]{0:T(128)} %lens_in.1, s32[2]{0:T(128)} %pids_in.1), custom_call_target="tpu_custom_call" | custom-call | tf_op jit(solution)/shard_map/gather_score/pallas_call | solution.py:465
  68.2 0.6 copy.10
  68.8 0.5 copy.11

commit v7 on v6

--- a/solution.py
+++ b/solution.py
@@ -30,7 +30,7 @@
     return min(off % n, -off % n)
 
 
-def plan(ny, nz, sizes, depth=0.8, rate=46.6e3, lag=2.4, least=(12, 8), most=16, tail=24):
+def plan(ny, nz, sizes, depth=1.2, rate=46.6e3, lag=2.2, least=(12, 8), most=16, tail=24):
     parts = {"a": (0, ny, nz), "b": (1, nz, ny), "c": (0, ny, nz)}
     groups = [(dy % ny, dz % nz) for dy in ring_offsets(ny) for dz in ring_offsets(nz)]
     now, free, pending, issued, arrive = [0.0], {}, {}, {}, {}
@@ -49,7 +49,7 @@
                 free[link] = start + sizes[colour] / rate
                 arrive[event] = max(arrive.get(event, 0.0), free[link] + lag)
                 issued[event] = issued.get(event, 0) + 1
-                ops.append(("send", link, event, what))
+                ops.append(("send", link, event, what, colour))
                 now[0] += 0.015
 
     def place(colour, off1, off2):
@@ -64,8 +64,8 @@
     def put1(colour, d, way):
         swap, n1, n2 = parts[colour]
         if d <= n1 // 2 and way in ways(n1, d):
-            event = ("p1", colour, d)
-            need[event] = len(ways(n1, d))
+            event = ("p1", both[colour], d)
+            need[event] = len(ways(n1, d)) * len(both[colour])
             outstanding.add(event)
             queue(("zy" if swap else "yz")[0] + "+-"[way < 0], n1 // 2 - d + n2 // 2 + extra[colour], colour, event,
                   place(colour, -way * (d - 1), 0))
@@ -76,14 +76,15 @@
             return
         if 2 * d == n2 and way != (1 if j % 4 in (0, 3) else -1):
             return
-        event = ("p2", colour, j, d)
-        need[event] = 2 if 2 * d < n2 else 1
+        event = ("p2", both[colour], j, d)
+        need[event] = (2 if 2 * d < n2 else 1) * len(both[colour])
         outstanding.add(event)
         queue(("zy" if swap else "yz")[1] + "+-"[way < 0], n2 // 2 - d + extra[colour], colour, event,
               place(colour, ring_offsets(n1)[j], -way * (d - 1)))
 
     have = {c: set() for c in "abc"}
     batch, done = {}, []
+    both = {"a": "ab", "b": "ab", "c": "c"}
 
     def got(colour, new):
         have[colour].update(new)
@@ -97,15 +98,17 @@
                     queue("x" + way, 1, "c", event, g)
 
     def take(event):
-        kind = event[0]
-        if kind == "x1":
+        if event[0] == "x1":
             for n, g in enumerate(batch[event]):
                 queue("x" + "+-"[(n + len(done)) % 2], 0, "c", ("x2", g), g)
             done.append(event)
             return
-        colour = event[1]
+        for colour in event[1]:
+            pass_on(event, colour)
+
+    def pass_on(event, colour):
         swap, n1, n2 = parts[colour]
-        if kind == "p1":
+        if event[0] == "p1":
             d = event[2]
             for way in ways(n1, d):
                 put1(colour, d + 1, way)
@@ -291,7 +294,7 @@
         n = tiles_of[colour]
         return store[colour].at[pl.ds(flat[g] * n, n)]
 
-    def put(link, event, g):
+    def put(link, event, g, colour):
         name, pos, n = axis[link[0]]
         dev = {name: at(pos, 1 if link[1] == "+" else -1, n)}
         side_in = "+-".index(link[1])
@@ -302,11 +305,12 @@
             here, there = cbuf.at[pl.ds(in_c(side_in, g), kq)], cbuf.at[pl.ds(in_c(2, g), kq)]
             send(here, there, c_send, d_recv.at[part_of[g]], dev, keep=False)
         else:
-            b = block(event[1], g)
-            send(b, b, out_sem[event[1]], e_recv.at[index[event]], dev, keep=False)
+            b = block(colour, g)
+            send(b, b, out_sem[colour], e_recv.at[index[event]], dev, keep=False)
 
     def get(event):
-        take_tiles(need[event] * tiles_of["c" if event[0] == "x1" else event[1]], e_recv.at[index[event]])
+        kinds = "c" if event[0] == "x1" else event[1]
+        take_tiles(need[event] * sum(tiles_of[k] for k in kinds) // len(kinds), e_recv.at[index[event]])
 
     wide = 2 * LANES
     chip = ((y * nz + z) * nx + x) * 2

time: 69.4 us -> 68.5 us (0.987)
  Pallas kernels: 67.6 us -> 66.7 us
    pallas_call x1, Pallas kernels: 67.6 us -> 66.7 us  [local(): pl.pallas_call(functools.partial(kernel, (nx, ny, nz, ka, kb, kq), steps,...]
where the time goes in v7:
time: 68.5 us; the launch traced here: 68.4 us
  Pallas kernels  66.7 us (97%)
  local copies, waits for them, and re-layouts  1.08 us (2%)
    pallas_call x1, Pallas kernels, local(): pl.pallas_call(functools.partial(kernel, (nx, ny, nz, ka, kb, kq), steps,...  66.7 us

profile of v7, /device:TPU:2, one launch (start us, length us, event | category | flops | bytes accessed | tf_op | source)
XLA Modules:
  0.0 68.4 jit_solution(7810279754996810690)
XLA Ops:
  0.6 66.7 %gather_score.1 = (f32[2,2]{1,0:T(2,128)S(1)}, f32[1,2]{1,0:T(1,128)S(1)}) custom-call(bf16[2,2,3584]{2,1,0:T(2,128)(2,1)} %hid_in.1, bf16[3584,384]{1,0:T(8,128)(2,1)} %whbm.1, bf16[28,128]{1,0:T(8,128)(2,1)} %bitcast.3, s32[2,2]{1,0:T(2,128)} %ids_in.1, s32[2]{0:T(128)} %lens_in.1, s32[2]{0:T(128)} %pids_in.1), custom_call_target="tpu_custom_call" | custom-call | tf_op jit(solution)/shard_map/gather_score/pallas_call | solution.py:469
  67.3 0.6 copy.10
  67.9 0.5 copy.11
